TPU v7x, 256 devices: a whole 4x4x8 slice. The times are simulated.
256 devices in a mesh: seq: 64 (over x, z, core), head: 4 (over y).
Axes of the slice: x: 4, y: 4, z: 8, core: 2. Of those that a mesh axis runs over, the one named last changes fastest.
Arguments:
- stream: bfloat16 [32768, 5120], P('seq', 'head'), may hold values from -6 to 6
- gate_input: bfloat16 [32768, 5120], P('seq', 'head'), may hold values from -6 to 6
- in_coeff: bfloat16 [32768, 128], P('seq'), may hold values from -0.5 to 0.5
- out_coeff: bfloat16 [32768, 128], P('seq'), may hold values from -0.5 to 0.5
- step_raw: float32 [80, 32768], P('head', 'seq'), may hold values from -4 to 4
- step_bias: float32 [80], P('head'), may hold values from -1 to 1
- decay_rate: float32 [80], P('head'), may hold values from 3.0517578e-05 to 0.05
- skip_scale: float32 [80], P('head'), may hold values from 0.5 to 5
- norm_gain: float32 [5120], P('head'), may hold values from 0.1 to 1.9
- out_proj: bfloat16 [5120, 2560], P('head'), may hold values from -0.078125 to 0.078125
- doc_starts: int32 [128], replicated, may hold values from 0 to 32767, as said below
Outputs:
- layer_out: bfloat16 [32768, 2560], P(('seq', 'head'))
Inputs may be any that keep to these rules, and one draw needn't show every extreme that they name: `doc_starts`: the first entry is 0, the last is 32767, and the entries strictly increase; entry i is the position where document i begins.
All inputs are finite; a program needn't handle non-finite values.
Results may differ from a plain program's by a relative error of at most 0.01.
Values may be sent and summed in bfloat16 or wider, within the bound.
A program may use at most 128 MiB of HBM per device.

v0:
```python
import jax
import jax.numpy as jnp
from jax import lax
from jax.sharding import Mesh
from jax.sharding import PartitionSpec as P

DI = 5120
BLOCK = 256
SEQ = ("seq_0", "seq_1", "seq_2")
SEQ_HEAD = ("seq_0", "seq_1", "seq_2", "head")


EPSILON = 1e-05


def neutral_like(value, identity):
    return jax.tree.map(
        lambda a, e: jnp.broadcast_to(jnp.asarray(e, a.dtype), a.shape), value, identity
    )


def prefix_by_axis(value, axes, combine, identity):
    before = start = neutral_like(value, identity)
    total = value
    for axis in reversed(axes):
        devices, place = (lax.axis_size(axis), lax.axis_index(axis))
        pieces = jax.tree.map(lambda part: lax.all_gather(part, axis), total)
        inside, total = (start, start)
        for k in range(devices):
            passed = k < place
            total = combine(total, jax.tree.map(lambda part: part[k], pieces))
            inside = jax.tree.map(lambda new, old: jnp.where(passed, new, old), total, inside)
        before = combine(inside, before)
    return before


def from_everyone(value, axis):
    devices = lax.axis_size(axis)
    return lax.all_to_all(
        jnp.broadcast_to(value[None], (devices, *value.shape)), axis, 0, 0, tiled=True
    )


def taken_together(value, axis):
    return from_everyone(value, axis).sum(axis=0)


def split_up(value, dim, devices):
    shape = value.shape
    pieces = value.reshape(*shape[:dim], devices, shape[dim] // devices, *shape[dim + 1 :])
    return jnp.moveaxis(pieces, dim, 0)


def sent_and_summed(value, axis, dim):
    devices = lax.axis_size(axis)
    pieces = lax.all_to_all(split_up(value, dim, devices), axis, 0, 0, tiled=True)
    return jnp.sum(pieces.astype(jnp.float32), axis=0)


def block_pass(carry_state, block_piece, want_output):
    stream_blk, in_blk, out_blk, step_blk, log_blk, doc_blk, before = block_piece
    head_count = step_blk.shape[0]
    span = step_blk.shape[1]
    head_size = stream_blk.shape[1] // head_count
    index_row = lax.iota(jnp.int32, span)
    upper_ones = (index_row[:, None] <= index_row[None, :]).astype(jnp.float32)
    cumulative = jnp.dot(log_blk, upper_ones)
    last_cum = cumulative[:, -1]
    same_end = (doc_blk == doc_blk[-1]).astype(jnp.float32)
    end_weight = (
        jnp.exp(jnp.minimum(last_cum[:, None] - cumulative, 0.0)) * step_blk * same_end[None, :]
    )
    scaled_in = (end_weight[:, :, None] * in_blk.astype(jnp.float32)[None, :, :]).astype(
        jnp.bfloat16
    )
    values = stream_blk.reshape(span, head_count, head_size)
    fresh_state = jnp.einsum("hsn,shp->hnp", scaled_in, values, preferred_element_type=jnp.float32)
    joined = doc_blk == before
    carry_gate = jnp.where(joined[-1], jnp.exp(last_cum), 0.0)
    new_state = carry_gate[:, None, None] * carry_state + fresh_state
    if not want_output:
        return (new_state, None)
    scores = jnp.dot(out_blk, in_blk.T, preferred_element_type=jnp.float32)
    live_pairs = (doc_blk[:, None] == doc_blk[None, :]) & (index_row[:, None] >= index_row[None, :])
    decay_pairs = jnp.where(
        live_pairs[None],
        jnp.exp(jnp.minimum(cumulative[:, :, None] - cumulative[:, None, :], 0.0)),
        0.0,
    )
    weights = (scores[None] * decay_pairs * step_blk[:, None, :]).astype(jnp.bfloat16)
    within = jnp.einsum("hts,shp->thp", weights, values, preferred_element_type=jnp.float32)
    carried = jnp.einsum("tn,hnp->thp", out_blk.astype(jnp.float32), carry_state)
    factor = jnp.where(joined[None, :], jnp.exp(cumulative), 0.0)
    output = within + factor.T[:, :, None] * carried
    return (new_state, output)


def state_step(carry_state, block_piece):
    return block_pass(carry_state, block_piece, False)


def full_step(carry_state, block_piece):
    return block_pass(carry_state, block_piece, True)


def combine_pair(earlier, later):
    return (earlier[0] * later[0], later[0][:, None, None] * earlier[1] + later[1])


def chain(shard_link, summary):
    identity = (jnp.ones_like(shard_link), jnp.zeros_like(summary))
    prior = prefix_by_axis((shard_link, summary), SEQ, combine_pair, identity)
    return prior[1]


def correction(log_decay, joined, out_coeff, incoming):
    shard_cum = jnp.cumsum(log_decay, axis=1)
    factor = jnp.where(joined[None, :], jnp.exp(shard_cum), 0.0)
    carried = jnp.einsum("tn,hnp->thp", out_coeff.astype(jnp.float32), incoming)
    return factor.T[:, :, None] * carried


def local(
    stream,
    gate_input,
    in_coeff,
    out_coeff,
    step_raw,
    step_bias,
    decay_rate,
    skip_scale,
    norm_gain,
    out_proj,
    doc_starts,
):
    row_count = stream.shape[0]
    channels = stream.shape[1]
    head_count = step_raw.shape[0]
    head_size = channels // head_count
    state_size = in_coeff.shape[1]
    block_count = row_count // BLOCK
    shard_index = lax.axis_index(SEQ)
    offset = shard_index * row_count
    position = offset + lax.iota(jnp.int32, row_count)
    doc_ids = jnp.sum((doc_starts[None, :] <= position[:, None]).astype(jnp.int32), axis=1) - 1
    before = jnp.sum((doc_starts <= offset - 1).astype(jnp.int32)) - 1
    step_size = jax.nn.softplus(step_raw + step_bias[:, None])
    log_decay = -step_size * decay_rate[:, None]
    block_docs = doc_ids.reshape(block_count, BLOCK)
    block_before = jnp.concatenate([before[None], block_docs[:-1, -1]])
    pieces = (
        stream.reshape(block_count, BLOCK, channels),
        in_coeff.reshape(block_count, BLOCK, state_size),
        out_coeff.reshape(block_count, BLOCK, state_size),
        step_size.reshape(head_count, block_count, BLOCK).transpose(1, 0, 2),
        log_decay.reshape(head_count, block_count, BLOCK).transpose(1, 0, 2),
        block_docs,
        block_before,
    )
    zero_state = jnp.zeros((head_count, state_size, head_size), jnp.float32)
    joined = doc_ids == before
    shard_link = jnp.where(joined[-1], jnp.exp(jnp.sum(log_decay, axis=1)), 0.0)
    summary, unused = lax.scan(state_step, zero_state, pieces)
    incoming = chain(shard_link, summary)
    last_state, outputs = lax.scan(full_step, zero_state, pieces)
    ssm_out = outputs.reshape(row_count, head_count, head_size) + correction(
        log_decay, joined, out_coeff, incoming
    )
    ssm_out = ssm_out + skip_scale[None, :, None] * stream.reshape(
        row_count, head_count, head_size
    ).astype(jnp.float32)
    gated = ssm_out.reshape(row_count, channels) * jax.nn.silu(gate_input.astype(jnp.float32))
    square_sum = taken_together(jnp.sum(gated * gated, axis=1), "head")
    scale_row = lax.rsqrt(square_sum / DI + EPSILON)
    hidden = (gated * scale_row[:, None] * norm_gain[None, :]).astype(jnp.bfloat16)
    summed = sent_and_summed(
        jnp.dot(hidden, out_proj, preferred_element_type=jnp.float32).astype(jnp.bfloat16),
        "head",
        0,
    )
    return summed.astype(jnp.bfloat16)


def solution(mesh):
    split = Mesh(
        mesh.devices.reshape(4, 8, 2, mesh.shape["head"]), ("seq_0", "seq_1", "seq_2", "head")
    )
    in_specs = (
        P(SEQ, "head"),
        P(SEQ, "head"),
        P(SEQ, None),
        P(SEQ, None),
        P("head", SEQ),
        P("head"),
        P("head"),
        P("head"),
        P("head"),
        P("head", None),
        P(),
    )
    out_specs = P(SEQ_HEAD, None)
    return jax.shard_map(local, mesh=split, in_specs=in_specs, out_specs=out_specs, check_vma=False)
```

profile of v0, /device:TPU:8, one launch (start us, length us, event | category | flops | bytes accessed | tf_op | source)
XLA Modules:
  0.0 283.6 jit_solution(16058988615829512872)
XLA Ops:
  8.2 1.3 fusion.132
  12.4 1.6 copy.51
  14.0 1.3 pad_add_fusion
  15.4 13.8 %while.25 = (s32[]{:T(128)}, f32[20,128,64]{1,2,0:T(8,128)S(1)}, s32[2,256]{1,0:T(2,128)S(1)}, s32[2]{0:T(128)}, bf16[2,20,256]{2,1,0:T(8,128)(2,1)}, /*index=5*...) while((s32[]{:T(128)}, f32[20,128,64]{1,2,0:T(8,128)S(1)}, ...), condition=%wide.region_8.9_spmd.clone, body=%wide.region_7.8_spmd.clone.sunk | while | flops 88429080 | bytes 3722917 | solution.py:163
  18.7 1.3 dynamic_slice.114
  25.6 1.3 dynamic_slice.114
  34.1 2.4 all-reduce
  36.7 11.1 %all-gather.12.cloned.1.call-done = f32[40,128,64]{1,2,0:T(8,128)} async-done(((f32[20,128,64]{1,2,0:T(8,128)}), f32[40,128,64]{1,2,0:T(8,128)}) %all-gather.12.cloned.1.call-update) | async-done | bytes 1310736 | tf_op jit(solution)/shard_map/all_gather | solution.py:27
  47.8 2.3 bitcast_add_fusion.8
  50.2 17.5 %all-reduce.1 = f32[160]{0:T(256)S(1)} all-reduce(f32[160]{0:T(256)S(1)} %get-tuple-element.291), channel_id=4, replica_groups=mesh['seq_0'=4,'seq_1'=8,'seq_2'=2,'head'=4] {'seq_1'}, use_global_device_ids=true, to_apply=%add.1 | all-reduce | flops 160 | bytes 1280
  67.8 48.4 %all-gather.8.cloned.1.call-done = f32[8,20,128,64]{2,3,1,0:T(8,128)} async-done(((f32[1,20,128,64]{2,3,1,0:T(8,128)}), f32[8,20,128,64]{2,3,1,0:T(8,128)}) %all-gather.8.cloned.1.call-update) | async-done | bytes 5242896 | tf_op jit(solution)/shard_map/all_gather | solution.py:27
  116.2 3.8 %multiply_add_fusion = f32[1,20,128,64]{2,3,1,0:T(8,128)} fusion(f32[8,20,128,64]{2,3,1,0:T(8,128)} %all-gather.8.cloned.1.call-done, f32[20]{0:T(128)S(1)} %get-tuple-element.284, f32[20]{0:T(128)S(1)} %get-tuple-element.289, f32[20]{0:T(128)S(1)} %get-tuple-element.288, f32[20]{0:T(128)S(1)} %get-tuple-element.287, f32[20]{0:T(128)S(1)} %get-tuple-element.286, ...), kind=kLoop, calls=%fused_computation.129 | loop fusion | flops 2457600 | bytes 5898880 | tf_op jit(solution)/shard_map/add | solution.py:107
  120.1 78.2 %while.24 = (s32[]{:T(128)}, f32[20,128,64]{1,2,0:T(8,128)S(1)}, f32[2,256,20,64]{1,0,3,2:T(2,128)}, s32[2,256]{1,0:T(2,128)S(1)}, s32[2]{0:T(128)}, /*index=5*/...) while((s32[]{:T(128)}, f32[20,128,64]{1,2,0:T(8,128)S(1)}, ...), condition=%wide.region_3.4_spmd.clone, body=%wide.region_2.3_spmd.clone.sunk | while | flops 365586464 | bytes 16479678 | solution.py:165
  121.0 1.3 dynamic_slice.108
  129.0 1.7 fusion.175
  130.7 1.3 copy.71
  132.1 27.1 %dynamic_update_slice.6 = f32[2,256,20,64]{1,0,3,2:T(2,128)} dynamic-update-slice(f32[2,256,20,64]{1,0,3,2:T(2,128)} %get-tuple-element.429, f32[1,256,20,64]{1,0,3,2:T(1,128)S(1)} %copy.71, s32[]{:T(128)S(6)} %copy.76, s32[]{:T(128)} %constant.49.clone.1..sunk, s32[]{:T(128)} %constant.49.clone.1..sunk, s32[]{:T(128)} %constant.49.clone.1..sunk) | dynamic-update-slice | bytes 2621444 | tf_op jit(solution)/shard_map/while/body/jit(dynamic_update_index_in_dim)/dynamic_update_slice | solution.py:165
  160.1 1.3 dynamic_slice.108
  168.1 1.7 fusion.175
  169.8 1.3 copy.71
  171.2 27.0 %dynamic_update_slice.6 = f32[2,256,20,64]{1,0,3,2:T(2,128)} dynamic-update-slice(f32[2,256,20,64]{1,0,3,2:T(2,128)} %get-tuple-element.429, f32[1,256,20,64]{1,0,3,2:T(1,128)S(1)} %copy.71, s32[]{:T(128)S(6)} %copy.76, s32[]{:T(128)} %constant.49.clone.1..sunk, s32[]{:T(128)} %constant.49.clone.1..sunk, s32[]{:T(128)} %constant.49.clone.1..sunk) | dynamic-update-slice | bytes 2621444 | tf_op jit(solution)/shard_map/while/body/jit(dynamic_update_index_in_dim)/dynamic_update_slice | solution.py:165
  198.2 2.9 %copy.58 = f32[512,1280]{0,1:T(8,128)} copy(bf16[512,1280]{1,0:T(8,128)(2,1)} %param.15) | data formatting | bytes 3932160 | tf_op jit(solution)/shard_map/convert_element_type | solution.py:171
  201.3 3.6 %reshape.255 = f32[512,20,64]{0,2,1:T(8,128)S(1)} reshape(f32[2,256,20,64]{1,0,3,2:T(2,128)} %get-tuple-element.99) | data formatting | bytes 5242880 | tf_op jit(solution)/shard_map/reshape | solution.py:166
  204.9 1.2 reduce-window.6
  206.5 9.8 %all-gather.3 = f32[4,1,20]{2,1,0:T(1,128)S(1)} all-gather(f32[1,1,20]{2,1,0:T(1,128)S(1)} %fusion.134), channel_id=1, replica_groups=mesh['seq_0'=4,'seq_1'=8,'seq_2'=2,'head'=4] {'seq_0'}, dimensions={0}, use_global_device_ids=true | all-gather | bytes 400 | tf_op jit(solution)/shard_map/all_gather | solution.py:27
  216.5 7.7 %fusion.44 = f32[512,20,64]{0,2,1:T(8,128)} fusion(f32[512,20,64]{0,2,1:T(8,128)S(1)} %reshape.255, f32[512,20,64]{0,2,1:T(8,128)} %bitcast.257, f32[20]{0:T(128)S(1)} %copy-done.26, f32[512,20]{0,1:T(8,128)S(1)} %select_bitcast_fusion.1, f32[4,20,128,64]{2,3,1,0:T(8,128)} %all-gather.10.cloned.1.call-done, ...), kind=kOutput, calls=%fused_computation.74 | convolution fusion | flops 177438720 | bytes 17212766 | tf_op jit(solution)/shard_map/tn,hnp->thp/dot_general | solution.py:119
  224.2 2.1 copy.59
  226.4 2.2 multiply_reduce_fusion
  228.6 8.5 %all_to_all.11 = f32[4,1,512]{2,1,0:T(1,128)S(1)} all-to-all(f32[4,1,512]{2,1,0:T(1,128)S(1)} %broadcast_in_dim.75), channel_id=1, replica_groups=mesh['seq_0'=4,'seq_1'=8,'seq_2'=2,'head'=4] {'head'}, dimensions={0} | all-to-all | bytes 16384 | tf_op jit(solution)/shard_map/all_to_all | solution.py:39
  237.1 7.4 %convolution_convert_fusion = bf16[512,2560]{1,0:T(8,128)(2,1)S(1)} fusion(bf16[1280,2560]{1,0:T(8,128)(2,1)} %param.24, f32[1280]{0:T(1024)S(1)} %copy-done.25, f32[512]{0:T(512)S(1)} %add_rsqrt_fusion, f32[512,1280]{1,0:T(8,128)S(1)} %copy.59, bf16[512,1280]{1,0:T(8,128)(2,1)} %param.16), kind=kOutput, calls=%fused_computation.65 | convolution fusion | flops 3362652160 | bytes 13114368 | tf_op jit(solution)/shard_map/dot_general | solution.py:177
  244.5 31.1 %all_to_all.12 = bf16[4,128,2560]{2,1,0:T(8,128)(2,1)S(1)} all-to-all(bf16[4,128,2560]{2,1,0:T(8,128)(2,1)S(1)} %bitcast.256), channel_id=1, replica_groups=mesh['seq_0'=4,'seq_1'=8,'seq_2'=2,'head'=4] {'head'}, dimensions={0} | all-to-all | bytes 5242880 | tf_op jit(solution)/shard_map/all_to_all | solution.py:56
  275.6 1.4 reduce_sum.62
  (153 shorter events, 32.1 us)
Async XLA Ops:
  6.5 8.8 %copy-start = (bf16[512,128]{1,0:T(8,128)(2,1)S(1)}, bf16[512,128]{1,0:T(8,128)(2,1)}, u32[]{:S(2)}) copy-start(bf16[512,128]{1,0:T(8,128)(2,1)} %param.17) | copy-start | bytes 393220
  6.5 41.3 %all-gather.12.cloned.1.call-start = ((), (), s32[]{:S(2)}) async-start(), calls=%async_computation.4 | async-start | bytes 1966080 | tf_op jit(solution)/shard_map/all_gather | solution.py:27
  11.1 4.2 %copy-start.3 = (f32[20,512]{1,0:T(8,128)}, f32[20,512]{1,0:T(8,128)S(1)}, u32[]{:S(2)}) copy-start(f32[20,512]{1,0:T(8,128)S(1)} %get-tuple-element.276) | copy-start | bytes 122884
  15.4 14.7 %copy-start.28 = (u32[256]{0:T(256)S(1)}, u32[256]{0:T(256)}, u32[]{:S(2)}) copy-start(u32[256]{0:T(256)} %constant.101) | copy-start | bytes 3076
  15.4 15.4 %copy-start.27 = (u32[256]{0:T(256)S(1)}, u32[256]{0:T(256)}, u32[]{:S(2)}) copy-start(u32[256]{0:T(256)} %constant.96) | copy-start | bytes 3076
  29.2 0.8 copy-start.2
  30.0 86.2 %all-gather.8.cloned.1.call-start = ((), (), s32[]{:S(2)}) async-start(), calls=%async_computation.2 | async-start | bytes 5898240 | tf_op jit(solution)/shard_map/all_gather | solution.py:27
  32.7 83.5 %copy-start.19 = (pred[512]{0:T(512)(128)(4,1)}, pred[512]{0:T(512)(128)(4,1)S(1)}, u32[]{:S(2)}) copy-start(pred[512]{0:T(512)(128)(4,1)S(1)} %broadcast_compare_fusion.1) | copy-start | bytes 1540
  36.7 79.5 %copy-start.21 = (f32[20]{0:T(128)}, f32[20]{0:T(128)S(1)}, u32[]{:S(2)}) copy-start(f32[20]{0:T(128)S(1)} %get-tuple-element.292) | copy-start | bytes 244
  36.7 79.5 %copy-start.23 = (f32[20]{0:T(128)}, f32[20]{0:T(128)S(1)}, u32[]{:S(2)}) copy-start(f32[20]{0:T(128)S(1)} %get-tuple-element.293) | copy-start | bytes 244
  50.1 166.3 %all-gather.10.cloned.1.call-start = ((), (), s32[]{:S(2)}) async-start(), calls=%async_computation.3 | async-start | bytes 3276800 | tf_op jit(solution)/shard_map/all_gather | solution.py:27
  67.7 52.2 %copy-start.5 = (f32[20]{0:T(128)}, f32[20]{0:T(128)S(1)}, u32[]{:S(2)}) copy-start(f32[20]{0:T(128)S(1)} %get-tuple-element.284) | copy-start | bytes 244
  67.7 52.2 %copy-start.7 = (f32[20]{0:T(128)}, f32[20]{0:T(128)S(1)}, u32[]{:S(2)}) copy-start(f32[20]{0:T(128)S(1)} %get-tuple-element.285) | copy-start | bytes 244
  67.7 52.2 %copy-start.9 = (f32[20]{0:T(128)}, f32[20]{0:T(128)S(1)}, u32[]{:S(2)}) copy-start(f32[20]{0:T(128)S(1)} %get-tuple-element.286) | copy-start | bytes 244
  67.8 52.2 %copy-start.11 = (f32[20]{0:T(128)}, f32[20]{0:T(128)S(1)}, u32[]{:S(2)}) copy-start(f32[20]{0:T(128)S(1)} %get-tuple-element.287) | copy-start | bytes 244
  67.8 52.2 %copy-start.13 = (f32[20]{0:T(128)}, f32[20]{0:T(128)S(1)}, u32[]{:S(2)}) copy-start(f32[20]{0:T(128)S(1)} %get-tuple-element.288) | copy-start | bytes 244
  67.8 52.2 %copy-start.15 = (f32[20]{0:T(128)}, f32[20]{0:T(128)S(1)}, u32[]{:S(2)}) copy-start(f32[20]{0:T(128)S(1)} %get-tuple-element.289) | copy-start | bytes 244
  67.8 52.2 %copy-start.17 = (f32[20]{0:T(128)}, f32[20]{0:T(128)S(1)}, u32[]{:S(2)}) copy-start(f32[20]{0:T(128)S(1)} %get-tuple-element.290) | copy-start | bytes 244
  116.2 3.8 %copy-start.1 = (bf16[512,128]{1,0:T(8,128)(2,1)S(1)}, bf16[512,128]{1,0:T(8,128)(2,1)}, u32[]{:S(2)}) copy-start(bf16[512,128]{1,0:T(8,128)(2,1)} %param.18) | copy-start | bytes 393220
  198.2 2.9 %copy-start.4 = (f32[20,512]{1,0:T(8,128)S(1)}, f32[20,512]{1,0:T(8,128)}, u32[]{:S(2)}) copy-start(f32[20,512]{1,0:T(8,128)} %copy-done.3) | copy-start | bytes 122884
  201.2 15.2 %copy-start.20 = (pred[512]{0:T(512)(128)(4,1)S(1)}, pred[512]{0:T(512)(128)(4,1)}, u32[]{:S(2)}) copy-start(pred[512]{0:T(512)(128)(4,1)} %copy-done.19) | copy-start | bytes 1540
  201.2 15.3 %copy-start.6 = (f32[20]{0:T(128)S(1)}, f32[20]{0:T(128)}, u32[]{:S(2)}) copy-start(f32[20]{0:T(128)} %copy-done.5) | copy-start | bytes 244
  201.2 15.3 %copy-start.8 = (f32[20]{0:T(128)S(1)}, f32[20]{0:T(128)}, u32[]{:S(2)}) copy-start(f32[20]{0:T(128)} %copy-done.7) | copy-start | bytes 244
  201.2 15.3 %copy-start.10 = (f32[20]{0:T(128)S(1)}, f32[20]{0:T(128)}, u32[]{:S(2)}) copy-start(f32[20]{0:T(128)} %copy-done.9) | copy-start | bytes 244
  201.2 15.3 %copy-start.12 = (f32[20]{0:T(128)S(1)}, f32[20]{0:T(128)}, u32[]{:S(2)}) copy-start(f32[20]{0:T(128)} %copy-done.11) | copy-start | bytes 244
  201.2 15.3 %copy-start.14 = (f32[20]{0:T(128)S(1)}, f32[20]{0:T(128)}, u32[]{:S(2)}) copy-start(f32[20]{0:T(128)} %copy-done.13) | copy-start | bytes 244
  201.2 15.3 %copy-start.16 = (f32[20]{0:T(128)S(1)}, f32[20]{0:T(128)}, u32[]{:S(2)}) copy-start(f32[20]{0:T(128)} %copy-done.15) | copy-start | bytes 244
  201.2 15.3 %copy-start.18 = (f32[20]{0:T(128)S(1)}, f32[20]{0:T(128)}, u32[]{:S(2)}) copy-start(f32[20]{0:T(128)} %copy-done.17) | copy-start | bytes 244
  201.2 15.3 %copy-start.22 = (f32[20]{0:T(128)S(1)}, f32[20]{0:T(128)}, u32[]{:S(2)}) copy-start(f32[20]{0:T(128)} %copy-done.21) | copy-start | bytes 244
  201.3 15.3 %copy-start.24 = (f32[20]{0:T(128)S(1)}, f32[20]{0:T(128)}, u32[]{:S(2)}) copy-start(f32[20]{0:T(128)} %copy-done.23) | copy-start | bytes 244
  201.3 15.3 %copy-start.26 = (f32[20]{0:T(128)S(1)}, f32[20]{0:T(128)}, u32[]{:S(2)}) copy-start(f32[20]{0:T(128)} %param.22) | copy-start | bytes 244
  226.3 10.7 %copy-start.25 = (f32[1280]{0:T(1024)S(1)}, f32[1280]{0:T(1024)}, u32[]{:S(2)}) copy-start(f32[1280]{0:T(1024)} %param.23) | copy-start | bytes 15364
Sparse Core Ops, SparseCore 0:
  30.2 17.6 all-gather.11
  50.3 65.9 all-gather.7
  120.2 36.1 all-gather.9
where the time goes:
time: 288 us; the launch traced here: 284 us
  local copies, waits for them, and re-layouts  82 us (28%)
  blocking collectives  69.3 us (24%)
  waiting for transfers between devices  59.6 us (21%)
  other arithmetic  27.1 us (9%)
  matrix products  27 us (9%)
  between operations  15.6 us (5%)
    all_gather x3, waiting for transfers between devices, prefix_by_axis(): pieces = jax.tree.map(lambda part: lax.all_gather(part, axis), total)  59.5 us
    dynamic_update_slice x4, local copies, waits for them, and re-layouts, local(): last_state, outputs = lax.scan(full_step, zero_state, pieces)  56.8 us
    all_to_all x1, blocking collectives, sent_and_summed(): lax.all_to_all(split_up(value, dim, devices), axis, 0, 0, tiled=True)  31.1 us
    unnamed x2, blocking collectives  19.9 us
    all_gather x1, blocking collectives, prefix_by_axis(): pieces = jax.tree.map(lambda part: lax.all_gather(part, axis), total)  9.81 us
    all_to_all x1, blocking collectives, from_everyone(): lax.all_to_all(jnp.broadcast_to(value[None], (devices, *value.shape)), ax...  8.47 us
    dot_general x1, matrix products, correction(): carried = jnp.einsum('tn,hnp->thp', out_coeff.astype(jnp.float32), incoming)  7.67 us
    dot_general x1, matrix products, local(): jnp.dot(hidden, out_proj, preferred_element_type=jnp.float32)  7.4 us
  transfers between devices with their start and end apart: 3, of which 2 were waited for; matrix products, arithmetic and copies ran while one was open for 31% of the time, Pallas kernels for 0%

commit v1 on v0

v1 whole, which is shorter than its diff:
```python
import functools

import jax
import jax.numpy as jnp
from jax import lax
from jax.experimental import pallas as pl
from jax.experimental.pallas import tpu as pltpu
from jax.sharding import PartitionSpec as P

DI = 5120
EPSILON = 1e-05
ROW = 16
LANE = 128
F32 = jnp.float32
BF16 = jnp.bfloat16
MESH = pl.DeviceIdType.MESH


def dot(a, b):
    return jnp.dot(a, b, preferred_element_type=F32)


def dot_nt(a, b):
    return lax.dot_general(a, b, (((1,), (1,)), ((), ())), preferred_element_type=F32)


def rounded(v):
    return v.astype(BF16).astype(F32)


def eye_mask(n):
    return lax.broadcasted_iota(jnp.int32, (n, n), 0) == lax.broadcasted_iota(jnp.int32, (n, n), 1)


def as_column(row, n):
    return jnp.sum(jnp.where(eye_mask(n), row, 0.0), axis=1, keepdims=True)


def as_row(column, n):
    return jnp.sum(jnp.where(eye_mask(n), column, 0.0), axis=0, keepdims=True)


def link_tile(row, rows):
    high = rounded(row)
    middle = rounded(row - high)
    low = row - high - middle
    at = lax.broadcasted_iota(jnp.int32, (rows, LANE), 0)
    return jnp.where(
        at == 0, high, jnp.where(at == 1, middle, jnp.where(at == 2, low, 0.0))
    ).astype(BF16)


def kernel(
    nx,
    nr,
    ny,
    x_hbm,
    g_hbm,
    b_hbm,
    c_hbm,
    st_hbm,
    bias_ref,
    rate_ref,
    skip_ref,
    gain_ref,
    w_hbm,
    doc_ref,
    out_ref,
    x_v,
    g_v,
    b_v,
    c_v,
    st_v,
    w_v,
    m_ref,
    mt_ref,
    e_ref,
    v_ref,
    sc_ref,
    cj_ref,
    a1_ref,
    a2_ref,
    row_ref,
    asend,
    arecv,
    ll_ref,
    lx_ref,
    pre_ref,
    pl_ref,
    xsend,
    xrecv,
    bsend,
    brecv,
    sp_ref,
    hid_ref,
    r1_send,
    r1_recv,
    r2_send,
    r2_recv,
    own_ref,
    ss_send,
    ss_recv,
    copy_sem,
    a_ssem,
    a_rsem,
    x_ssem,
    x_rsem,
    b_ssem,
    b_rsem,
    r1_ssem,
    r1_rsem,
    r2_ssem,
    r2_rsem,
    ss_ssem,
    ss_rsem,
):
    seq = lax.axis_index("seq")
    head = lax.axis_index("head")
    xi = seq // nr
    me = seq % nr
    tokens, channels = x_v.shape
    heads = st_v.shape[0]
    state = b_v.shape[1]
    width = w_v.shape[1]
    half = width // 2
    sr = state // nr
    part = tokens // ny
    offset = seq * tokens
    head_size = channels // heads

    loads = [
        pltpu.make_async_copy(src, dst, copy_sem.at[i])
        for i, (src, dst) in enumerate(
            (
                (st_hbm, st_v),
                (b_hbm, b_v),
                (x_hbm, x_v),
                (c_hbm, c_v),
                (g_hbm, g_v),
                (w_hbm, w_v),
            )
        )
    ]
    for load in loads:
        load.start()

    barrier = pltpu.get_barrier_semaphore()
    in_row = [(xi * nr + (me + k) % nr, head) for k in range(nr)]
    in_x = [(((xi + k) % nx) * nr + me, head) for k in range(nx)]
    in_y = [(seq, (head + k) % ny) for k in range(ny)]
    for device in in_row[1:] + in_x[1:] + in_y[1:]:
        pl.semaphore_signal(barrier, inc=1, device_id=device, device_id_type=MESH)

    e_ref[...] = (
        (lax.broadcasted_iota(jnp.int32, (LANE, channels), 0) & 31)
        == lax.broadcasted_iota(jnp.int32, (LANE, channels), 1) // head_size
    ).astype(F32).astype(BF16)
    m_ref[...] = jnp.zeros_like(m_ref)
    starts = doc_ref[...]
    position = offset + lax.broadcasted_iota(jnp.int32, (tokens, 1), 0)
    doc_start = jnp.max(
        jnp.where(starts <= position, starts.astype(F32), -1.0), axis=1, keepdims=True
    )
    joined = doc_start < offset.astype(F32)
    last_start = doc_start[tokens - 1 :, :]

    bias = as_column(bias_ref[...], heads)
    rate = as_column(rate_ref[...], heads)
    skip = as_column(skip_ref[...], heads)
    loads[0].wait()
    step = st_v[...] + bias
    step = jnp.maximum(step, 0.0) + jnp.log1p(jnp.exp(-jnp.abs(step)))
    cum = -step * rate
    lane = lax.broadcasted_iota(jnp.int32, (heads, tokens), 1)
    shift = 1
    while shift < tokens:
        cum = cum + jnp.where(lane >= shift, pltpu.roll(cum, shift, 1), 0.0)
        shift *= 2
    mid = cum[:, tokens // 2 - 1 : tokens // 2]
    total = cum[:, tokens - 1 :]
    before_scale = jnp.exp(mid - cum) * step
    after_scale = jnp.exp(cum - mid)

    def put(first, columns, value):
        high = rounded(value)
        m_ref[first : first + heads, columns] = high
        m_ref[first + 32 : first + 32 + heads, columns] = value - high

    wide = (heads, LANE)
    put(0, slice(0, tokens), before_scale)
    put(64, slice(0, tokens), after_scale)
    put(0, slice(tokens, tokens + LANE), jnp.broadcast_to(jnp.exp(mid), wide))
    put(64, slice(tokens, tokens + LANE), jnp.broadcast_to(skip, wide))
    mt_ref[...] = m_ref[...].T.astype(BF16)
    gate_row = jnp.where(last_start < offset.astype(F32), total, -1e30)
    link_row = jnp.sum(
        jnp.where(
            lax.broadcasted_iota(jnp.int32, (heads, LANE), 0)
            == lax.broadcasted_iota(jnp.int32, (heads, LANE), 1),
            gate_row,
            0.0,
        ),
        axis=0,
        keepdims=True,
    )

    def expand(rows, upper):
        block = mt_ref[rows, :]
        at = lax.broadcasted_iota(jnp.int32, block.shape, 1)
        block = jnp.where((at >= 64) if upper else (at < 64), block.astype(F32), 0.0)
        return block.astype(BF16)

    row_ref[0:8, :] = dot(expand(slice(tokens - 8, tokens), True), e_ref[...])
    row_ref[8:16, :] = dot(expand(slice(tokens, tokens + 8), False), e_ref[...])
    row_ref[16:24, :] = dot(expand(slice(tokens, tokens + 8), True), e_ref[...])

    loads[2].wait()
    step_rows = 128
    columns = [slice(c, c + 256) for c in range(0, channels, 256)]

    @pl.loop(0, tokens // step_rows)
    def _(i):
        rows = pl.ds(pl.multiple_of(i * step_rows, step_rows), step_rows)
        left = expand(rows, False)
        for cols in columns:
            v_ref[rows, cols] = (
                x_v[rows, cols].astype(F32) * dot(left, e_ref[:, cols])
            ).astype(BF16)

    loads[1].wait()
    kept = jnp.where(position.astype(F32) >= last_start, b_v[...].astype(F32), 0.0)
    kept = kept.T.astype(BF16)
    tile = link_tile(link_row, sr)
    for cols in columns:
        piece = dot(kept, v_ref[:, cols]) * row_ref[7:8, cols]
        for j in range(nr):
            asend[j, :, cols] = piece[j * sr : (j + 1) * sr, :].astype(BF16)
    for j in range(nr):
        asend[j, :, channels:] = tile

    pl.semaphore_wait(barrier, nr + nx + ny - 3)

    def around(n):
        order = []
        for d in range(n // 2, 0, -1):
            order += [d] if 2 * d == n else [d, n - d]
        return order

    row_copies = {}
    for k in around(nr):
        target = (me + k) % nr
        row_copies[k] = pltpu.make_async_remote_copy(
            src_ref=asend.at[target],
            dst_ref=arecv.at[me],
            send_sem=a_ssem.at[k - 1],
            recv_sem=a_rsem.at[k - 1],
            device_id=in_row[k],
            device_id_type=MESH,
        )
        row_copies[k].start()
    arecv[me] = asend[me]

    loads[3].wait()
    cj_ref[...] = jnp.where(joined, c_v[...].astype(F32), 0.0).astype(BF16)
    loads[4].wait()

    @pl.loop(0, tokens // step_rows)
    def _(i):
        first = pl.multiple_of(i * step_rows, step_rows)
        rows = pl.ds(first, step_rows)
        scores = dot_nt(c_v[rows, :], b_v[...])
        at = offset + first + lax.broadcasted_iota(jnp.int32, (step_rows, 1), 0)
        source = offset + lax.broadcasted_iota(jnp.int32, (step_rows, tokens), 1)
        begun = jnp.max(
            jnp.where(starts <= at, starts.astype(F32), -1.0), axis=1, keepdims=True
        )
        live = (source <= at) & (source.astype(F32) >= begun)
        sc_ref[...] = jnp.where(live, scores, 0.0).astype(BF16)
        left = expand(rows, True)
        for cols in columns:
            scale = dot(left, e_ref[:, cols])
            gate = g_v[rows, cols].astype(F32)
            gate = gate / (1.0 + jnp.exp(-gate))
            inside = dot(sc_ref[...], v_ref[:, cols])
            skipped = row_ref[16:17, cols] * x_v[rows, cols].astype(F32)
            a1_ref[rows, cols] = scale * gate
            a2_ref[rows, cols] = (scale * inside + skipped) * gate

    for k in around(nr):
        row_copies[k].wait_recv()

    def link_of(block):
        pieces = block[:, channels:].astype(F32)
        return jnp.sum(pieces, axis=0, keepdims=True)

    def spread(logs):
        at = lax.broadcasted_iota(jnp.int32, logs.shape, 1)
        value = jnp.where(at < heads, jnp.exp(logs), 0.0)
        high = value.astype(BF16)
        rest = value - high.astype(F32)
        middle = rest.astype(BF16)
        low = (rest - middle.astype(F32)).astype(BF16)
        return dot(high, e_ref[...]) + dot(middle, e_ref[...]) + dot(low, e_ref[...])

    for j in range(nr):
        ll_ref[j : j + 1, :] = link_of(arecv[j])
    row_log = jnp.sum(ll_ref[0:nr, :], axis=0, keepdims=True)
    lx_ref[0:nr, :] = spread(ll_ref[0:nr, :])
    prefix = jnp.zeros((sr, channels), F32)
    product = jnp.ones((1, channels), F32)
    for j in range(nr):
        pre_ref[j] = prefix
        pl_ref[j : j + 1, :] = product
        link = lx_ref[j : j + 1, :]
        prefix = link * prefix + arecv[j, :, 0:channels].astype(F32)
        product = product * link
    xsend[:, 0:channels] = prefix.astype(BF16)
    xsend[:, channels:] = link_tile(row_log, sr)

    x_copies = {}
    for k in around(nx):
        x_copies[k] = pltpu.make_async_remote_copy(
            src_ref=xsend,
            dst_ref=xrecv.at[xi],
            send_sem=x_ssem.at[k - 1],
            recv_sem=x_rsem.at[k - 1],
            device_id=in_x[k],
            device_id_type=MESH,
        )
        x_copies[k].start()
    xrecv[xi] = xsend[...]
    for k in around(nx):
        x_copies[k].wait_recv()
    for j in range(nx):
        ll_ref[j : j + 1, :] = link_of(xrecv[j])
    lx_ref[0:nx, :] = spread(ll_ref[0:nx, :])
    earlier = jnp.zeros((sr, channels), F32)
    for j in range(nx - 1):
        after = lx_ref[j : j + 1, :] * earlier + xrecv[j, :, 0:channels].astype(F32)
        earlier = jnp.where(j < xi, after, earlier)
    for j in range(nr):
        bsend[j] = (pre_ref[j] + pl_ref[j : j + 1, :] * earlier).astype(BF16)

    back_copies = {}
    for k in around(nr):
        target = (me + k) % nr
        back_copies[k] = pltpu.make_async_remote_copy(
            src_ref=bsend.at[target],
            dst_ref=brecv.at[me],
            send_sem=b_ssem.at[k - 1],
            recv_sem=b_rsem.at[k - 1],
            device_id=in_row[k],
            device_id_type=MESH,
        )
        back_copies[k].start()
    brecv[me] = bsend[me]
    for k in around(nr):
        back_copies[k].wait_recv()
    for j in range(nr):
        rows = slice(j * sr, (j + 1) * sr)
        sp_ref[rows, :] = (row_ref[8:9, :] * brecv[j].astype(F32)).astype(BF16)

    sends = [*row_copies.values(), *x_copies.values(), *back_copies.values()]

    def make_hidden(k):
        chunk = (head + k) % ny
        rows = pl.ds(pl.multiple_of(chunk * part, part), part)
        squares = jnp.zeros((part, 1), F32)
        for cols in columns:
            gated = a2_ref[rows, cols] + a1_ref[rows, cols] * dot(
                cj_ref[rows, :], sp_ref[:, cols]
            )
            squares = squares + jnp.sum(gated * gated, axis=1, keepdims=True)
            hid_ref[rows, cols] = (gated * gain_ref[:, cols]).astype(BF16)
        ss_send[k] = jnp.broadcast_to(as_row(squares, part), (8, part))
        if k:
            copy = pltpu.make_async_remote_copy(
                src_ref=ss_send.at[k],
                dst_ref=ss_recv.at[k - 1],
                send_sem=ss_ssem.at[k - 1],
                recv_sem=ss_rsem.at[k - 1],
                device_id=in_y[k],
                device_id_type=MESH,
            )
            copy.start()
            return copy

    def project(k, side, store):
        chunk = (head + k) % ny
        rows = pl.ds(pl.multiple_of(chunk * part, part), part)
        for c in range(0, half, 256):
            store(
                slice(c, c + 256),
                dot(hid_ref[rows, :], w_v[:, side * half + c : side * half + c + 256]),
            )

    def send(src, dst, ssem, rsem, device):
        copy = pltpu.make_async_remote_copy(
            src_ref=src,
            dst_ref=dst,
            send_sem=ssem,
            recv_sem=rsem,
            device_id=device,
            device_id_type=MESH,
        )
        copy.start()
        return copy

    def into(ref):
        def store(cols, value):
            ref[:, cols] = value.astype(BF16)

        return store

    def added(ref, extra):
        def store(cols, value):
            ref[:, cols] = (value + extra[:, cols].astype(F32)).astype(BF16)

        return store

    up, down = in_y[1], in_y[ny - 1]
    squares_sent = [make_hidden(2)]
    loads[5].wait()
    first = []
    for side, device in ((0, up), (1, down)):
        project(2, side, into(r1_send.at[side]))
        first.append(
            send(
                r1_send.at[side],
                r1_recv.at[side],
                r1_ssem.at[side],
                r1_rsem.at[side],
                device,
            )
        )
    second = []
    for side, k, device in ((0, 1, up), (1, ny - 1, down)):
        squares_sent.append(make_hidden(k))
        project(k, 1 - side, into(r2_send.at[side, 0]))
        second.append(
            send(
                r2_send.at[side, 0],
                r2_recv.at[side, 0],
                r2_ssem.at[side, 0],
                r2_rsem.at[side, 0],
                device,
            )
        )
    make_hidden(0)
    for side in (0, 1):

        def store(cols, value, side=side):
            own_ref[:, side * half + cols.start : side * half + cols.stop] = value

        project(0, side, store)
    for side, k, device in ((0, 1, up), (1, ny - 1, down)):
        first[side].wait_recv()
        project(k, side, added(r2_send.at[side, 1], r1_recv.at[side]))
        second.append(
            send(
                r2_send.at[side, 1],
                r2_recv.at[side, 1],
                r2_ssem.at[side, 1],
                r2_rsem.at[side, 1],
                device,
            )
        )
    for copy in squares_sent:
        copy.wait_recv()
    total_squares = ss_send[0]
    for k in range(ny - 1):
        total_squares = total_squares + ss_recv[k]
    scale = lax.rsqrt(as_column(total_squares[0:1, :], part) / DI + EPSILON)
    for copy in second[:2]:
        copy.wait_recv()
    for side in (0, 1):
        base = (1 - side) * half
        for c in range(0, half, 256):
            cols = slice(base + c, base + c + 256)
            own_ref[:, cols] = own_ref[:, cols] + r2_recv[side, 0, :, c : c + 256].astype(F32)
    for side in (0, 1):
        second[2 + side].wait_recv()
        base = side * half
        for c in range(0, half, 256):
            cols = slice(base + c, base + c + 256)
            value = own_ref[:, cols] + r2_recv[side, 1, :, c : c + 256].astype(F32)
            out_ref[:, cols] = (value * scale).astype(BF16)
    for copy in sends + squares_sent + first + second:
        copy.wait_send()


def local(nx, nr, ny, stream, gate, inc, outc, step_raw, bias, rate, skip, gain, proj, starts):
    tokens, channels = stream.shape
    heads = step_raw.shape[0]
    state = inc.shape[1]
    width = proj.shape[1]
    sr = state // nr
    part = tokens // ny
    anyspace = pl.BlockSpec(memory_space=pl.ANY)
    vmem = pl.BlockSpec(memory_space=pltpu.VMEM)
    dma = pltpu.SemaphoreType.DMA
    scratch = [
        pltpu.VMEM((tokens, channels), BF16),
        pltpu.VMEM((tokens, channels), BF16),
        pltpu.VMEM((tokens, state), BF16),
        pltpu.VMEM((tokens, state), BF16),
        pltpu.VMEM((heads, tokens), F32),
        pltpu.VMEM((channels, width), BF16),
        pltpu.VMEM((LANE, tokens + LANE), F32),
        pltpu.VMEM((tokens + LANE, LANE), BF16),
        pltpu.VMEM((LANE, channels), BF16),
        pltpu.VMEM((tokens, channels), BF16),
        pltpu.VMEM((128, tokens), BF16),
        pltpu.VMEM((tokens, state), BF16),
        pltpu.VMEM((tokens, channels), F32),
        pltpu.VMEM((tokens, channels), F32),
        pltpu.VMEM((24, channels), F32),
        pltpu.VMEM((nr, sr, channels + LANE), BF16),
        pltpu.VMEM((nr, sr, channels + LANE), BF16),
        pltpu.VMEM((16, LANE), F32),
        pltpu.VMEM((16, channels), F32),
        pltpu.VMEM((nr, sr, channels), F32),
        pltpu.VMEM((16, channels), F32),
        pltpu.VMEM((sr, channels + LANE), BF16),
        pltpu.VMEM((nx, sr, channels + LANE), BF16),
        pltpu.VMEM((nr, sr, channels), BF16),
        pltpu.VMEM((nr, sr, channels), BF16),
        pltpu.VMEM((state, channels), BF16),
        pltpu.VMEM((tokens, channels), BF16),
        pltpu.VMEM((2, part, width // 2), BF16),
        pltpu.VMEM((2, part, width // 2), BF16),
        pltpu.VMEM((2, 2, part, width // 2), BF16),
        pltpu.VMEM((2, 2, part, width // 2), BF16),
        pltpu.VMEM((part, width), F32),
        pltpu.VMEM((ny, 8, part), F32),
        pltpu.VMEM((ny - 1, 8, part), F32),
        dma((6,)),
        dma((nr - 1,)),
        dma((nr - 1,)),
        dma((nx - 1,)),
        dma((nx - 1,)),
        dma((nr - 1,)),
        dma((nr - 1,)),
        dma((2,)),
        dma((2,)),
        dma((2, 2)),
        dma((2, 2)),
        dma((ny - 1,)),
        dma((ny - 1,)),
    ]
    return pl.pallas_call(
        functools.partial(kernel, nx, nr, ny),
        out_shape=jax.ShapeDtypeStruct((part, width), BF16),
        in_specs=[anyspace] * 5 + [vmem] * 4 + [anyspace, vmem],
        out_specs=vmem,
        scratch_shapes=scratch,
        compiler_params=pltpu.CompilerParams(
            collective_id=0, has_side_effects=True, vmem_limit_bytes=56 * 1024 * 1024
        ),
        name="ssd_layer",
    )(
        stream,
        gate,
        inc,
        outc,
        step_raw,
        bias[None],
        rate[None],
        skip[None],
        gain[None],
        proj,
        starts[None],
    )


def solution(mesh):
    devices = mesh.shape["seq"]
    nr = min(ROW, devices // 2)
    in_specs = (
        P("seq", "head"),
        P("seq", "head"),
        P("seq", None),
        P("seq", None),
        P("head", "seq"),
        P("head"),
        P("head"),
        P("head"),
        P("head"),
        P("head", None),
        P(),
    )
    return jax.shard_map(
        functools.partial(local, devices // nr, nr, mesh.shape["head"]),
        mesh=mesh,
        in_specs=in_specs,
        out_specs=P(("seq", "head"), None),
        check_vma=False,
    )
```

time: 288 us -> 63.9 us (0.22)
  the two profiles are of different devices: /device:TPU:8 before, /device:TPU:1 now
where the time goes in v1:
time: 63.9 us; the launch traced here: 63.7 us
  Pallas kernels  60.4 us (95%)
  local copies, waits for them, and re-layouts  3.26 us (5%)
    pallas_call x1, Pallas kernels, local(): pl.pallas_call(functools.partial(kernel, nx, nr, ny), out_shape=jax.Shape...  60.4 us
    unnamed x1, local copies, waits for them, and re-layouts  1.97 us
    broadcast_in_dim x1, local copies, waits for them, and re-layouts, local(): gain[None]  1.29 us

profile of v1, /device:TPU:1, one launch (start us, length us, event | category | flops | bytes accessed | tf_op | source)
XLA Modules:
  0.0 63.7 jit_solution(11058234827067807553)
XLA Ops:
  0.0 1.3 %broadcast_in_dim.18.gain_ref = f32[1,1280]{1,0:T(1,128)} reshape(f32[1280]{0:T(1024)} %param.19) | data formatting | bytes 10240 | tf_op jit(solution)/shard_map/broadcast_in_dim | solution.py:570
  1.3 60.4 %ssd_layer.1 = bf16[128,2560]{1,0:T(8,128)(2,1)} custom-call(bf16[512,1280]{1,0:T(8,128)(2,1)} %x_hbm.1, bf16[512,1280]{1,0:T(8,128)(2,1)} %g_hbm.1, bf16[512,128]{1,0:T(8,128)(2,1)} %b_hbm.1, bf16[512,128]{1,0:T(8,128)(2,1)} %c_hbm.1, f32[20,512]{1,0:T(8,128)} %st_hbm.1, f32[1,20]{1,0:T(1,128)} %bitcast.4, f32[1,20]{1,0:T(1,128)} %bitcast.5, ...), custom_call_target="tpu_custom_call" | custom-call | tf_op jit(solution)/shard_map/ssd_layer/pallas_call | solution.py:551
  61.7 2.0 %copy.13 = bf16[128,2560]{1,0:T(8,128)(2,1)} copy(bf16[128,2560]{1,0:T(8,128)(2,1)} %ssd_layer.1) | data formatting | bytes 1310720

commit v2 on v1

v2 whole, which is shorter than its diff:
```python
import functools

import jax
import jax.numpy as jnp
from jax import lax
from jax.experimental import pallas as pl
from jax.experimental.pallas import tpu as pltpu
from jax.sharding import PartitionSpec as P

DI = 5120
EPSILON = 1e-05
ALONG_Z = 8
LANE = 128
F32 = jnp.float32
BF16 = jnp.bfloat16
MESH = pl.DeviceIdType.MESH


def dot(a, b):
    return jnp.dot(a, b, preferred_element_type=F32)


def dot_nt(a, b):
    return lax.dot_general(a, b, (((1,), (1,)), ((), ())), preferred_element_type=F32)


def rounded(v):
    return v.astype(BF16).astype(F32)


def eye_mask(n):
    return lax.broadcasted_iota(jnp.int32, (n, n), 0) == lax.broadcasted_iota(jnp.int32, (n, n), 1)


def as_column(row, n):
    return jnp.sum(jnp.where(eye_mask(n), row, 0.0), axis=1, keepdims=True)


def as_row(column, n):
    return jnp.sum(jnp.where(eye_mask(n), column, 0.0), axis=0, keepdims=True)


def link_tile(row, rows):
    high = rounded(row)
    middle = rounded(row - high)
    low = row - high - middle
    at = lax.broadcasted_iota(jnp.int32, (rows, LANE), 0)
    return jnp.where(
        at == 0, high, jnp.where(at == 1, middle, jnp.where(at == 2, low, 0.0))
    ).astype(BF16)


def kernel(
    nx,
    nz,
    ny,
    x_hbm,
    g_hbm,
    b_hbm,
    c_hbm,
    st_hbm,
    bias_ref,
    rate_ref,
    skip_ref,
    gain_ref,
    w_hbm,
    doc_ref,
    out_hbm,
    x_v,
    g_v,
    b_v,
    c_v,
    st_v,
    w_v,
    m_ref,
    mt_ref,
    e_ref,
    v_ref,
    sc_ref,
    cj_ref,
    a1_ref,
    a2_ref,
    row_ref,
    own_s,
    pair_send,
    pair_recv,
    first_s,
    asend,
    arecv,
    ll_ref,
    lx_ref,
    l0_ref,
    pre_ref,
    pl_ref,
    xsend,
    xrecv,
    bsend,
    brecv,
    fsend,
    frecv,
    sp_ref,
    hid_ref,
    r1_send,
    r1_recv,
    r2_send,
    r2_recv,
    own_ref,
    out_v,
    ss_send,
    ss_recv,
    copy_sem,
    p_sem,
    a_ssem,
    a_rsem,
    x_ssem,
    x_rsem,
    b_ssem,
    b_rsem,
    f_ssem,
    f_rsem,
    r1_ssem,
    r1_rsem,
    r2_ssem,
    r2_rsem,
    ss_ssem,
    ss_rsem,
    out_sem,
):
    seq = lax.axis_index("seq")
    head = lax.axis_index("head")
    core = seq % 2
    z = (seq // 2) % nz
    xi = seq // (2 * nz)
    is_first = core == 0
    tokens, channels = x_v.shape
    heads = st_v.shape[0]
    state = b_v.shape[1]
    width = w_v.shape[1]
    half = width // 2
    side_width = channels // 2
    sr = state // nz
    part = tokens // ny
    offset = seq * tokens
    head_size = channels // heads

    loads = [
        pltpu.make_async_copy(src, dst, copy_sem.at[i])
        for i, (src, dst) in enumerate(
            (
                (st_hbm, st_v),
                (b_hbm, b_v),
                (x_hbm, x_v),
                (c_hbm, c_v),
                (g_hbm, g_v),
                (w_hbm, w_v),
            )
        )
    ]
    for load in loads[:3]:
        load.start()

    barrier = pltpu.get_barrier_semaphore()
    partner = (seq + 1 - 2 * core, head)
    in_z = [((xi * nz + (z + k) % nz) * 2 + core, head) for k in range(nz)]
    in_x = [((((xi + k) % nx) * nz + z) * 2 + core, head) for k in range(nx)]
    in_y = [(seq, (head + k) % ny) for k in range(ny)]
    greeted = in_z[1:] + in_x[1:] + in_y[1:] + [partner]
    for device in greeted:
        pl.semaphore_signal(barrier, inc=1, device_id=device, device_id_type=MESH)

    def send(src, dst, ssem, rsem, device):
        copy = pltpu.make_async_remote_copy(
            src_ref=src,
            dst_ref=dst,
            send_sem=ssem,
            recv_sem=rsem,
            device_id=device,
            device_id_type=MESH,
        )
        copy.start()
        return copy

    def around(n):
        order = []
        for d in range(n // 2, 0, -1):
            order += [d] if 2 * d == n else [d, n - d]
        return order

    e_ref[...] = (
        (lax.broadcasted_iota(jnp.int32, (LANE, channels), 0) & 31)
        == lax.broadcasted_iota(jnp.int32, (LANE, channels), 1) // head_size
    ).astype(F32).astype(BF16)
    m_ref[...] = jnp.zeros_like(m_ref)
    ll_ref[...] = jnp.zeros_like(ll_ref)
    starts = doc_ref[...]
    position = offset + lax.broadcasted_iota(jnp.int32, (tokens, 1), 0)
    doc_start = jnp.max(
        jnp.where(starts <= position, starts.astype(F32), -1.0), axis=1, keepdims=True
    )
    joined = doc_start < offset.astype(F32)
    last_start = doc_start[tokens - 1 :, :]

    bias = as_column(bias_ref[...], heads)
    rate = as_column(rate_ref[...], heads)
    skip = as_column(skip_ref[...], heads)
    loads[0].wait()
    step = st_v[...] + bias
    step = jnp.maximum(step, 0.0) + jnp.log1p(jnp.exp(-jnp.abs(step)))
    cum = -step * rate
    lane = lax.broadcasted_iota(jnp.int32, (heads, tokens), 1)
    shift = 1
    while shift < tokens:
        cum = cum + jnp.where(lane >= shift, pltpu.roll(cum, shift, 1), 0.0)
        shift *= 2
    mid = cum[:, tokens // 2 - 1 : tokens // 2]
    total = cum[:, tokens - 1 :]
    before_scale = jnp.exp(mid - cum) * step
    after_scale = jnp.exp(cum - mid)

    def put(first, columns, value):
        high = rounded(value)
        m_ref[first : first + heads, columns] = high
        m_ref[first + 32 : first + 32 + heads, columns] = value - high

    wide = (heads, LANE)
    put(0, slice(0, tokens), before_scale)
    put(64, slice(0, tokens), after_scale)
    put(0, slice(tokens, tokens + LANE), jnp.broadcast_to(jnp.exp(mid), wide))
    put(64, slice(tokens, tokens + LANE), jnp.broadcast_to(skip, wide))
    mt_ref[...] = m_ref[...].T.astype(BF16)
    gate_row = jnp.where(last_start < offset.astype(F32), total, -1e30)
    link_row = jnp.sum(
        jnp.where(
            lax.broadcasted_iota(jnp.int32, (heads, LANE), 0)
            == lax.broadcasted_iota(jnp.int32, (heads, LANE), 1),
            gate_row,
            0.0,
        ),
        axis=0,
        keepdims=True,
    )

    def expand(rows, upper):
        block = mt_ref[rows, :]
        at = lax.broadcasted_iota(jnp.int32, block.shape, 1)
        block = jnp.where((at >= 64) if upper else (at < 64), block.astype(F32), 0.0)
        return block.astype(BF16)

    row_ref[0:8, :] = dot(expand(slice(tokens - 8, tokens), True), e_ref[...])
    row_ref[8:16, :] = dot(expand(slice(tokens, tokens + 8), False), e_ref[...])
    row_ref[16:24, :] = dot(expand(slice(tokens, tokens + 8), True), e_ref[...])

    step_rows = 128
    columns = [slice(c, c + 256) for c in range(0, channels, 256)]
    cuts = [(c, min(256, side_width - c)) for c in range(0, side_width, 256)]
    mine = core * side_width
    others = (1 - core) * side_width

    def lanes(base, cut):
        return pl.ds(pl.multiple_of(base + cut[0], LANE), cut[1])

    loads[1].wait()
    kept = jnp.where(position.astype(F32) >= last_start, b_v[...].astype(F32), 0.0)
    kept = kept.T.astype(BF16)
    loads[2].wait()
    for load in loads[3:]:
        load.start()

    def summary(base, store):
        @pl.loop(0, tokens // step_rows)
        def _(i):
            rows = pl.ds(pl.multiple_of(i * step_rows, step_rows), step_rows)
            left = expand(rows, False)
            for cut in cuts:
                cols = lanes(base, cut)
                v_ref[rows, cols] = (
                    x_v[rows, cols].astype(F32) * dot(left, e_ref[:, cols])
                ).astype(BF16)

        for cut in cuts:
            cols = lanes(base, cut)
            store(
                slice(cut[0], cut[0] + cut[1]),
                dot(kept, v_ref[:, cols]) * row_ref[7:8, cols],
            )

    def to_partner(cols, value):
        pair_send[0:state, cols] = value.astype(BF16)

    def to_own(cols, value):
        own_s[:, cols] = value

    pair_send[state:, :] = jnp.zeros((8, side_width), BF16)
    pair_send[state:, 0:LANE] = link_tile(link_row, 8)
    summary(others, to_partner)
    pl.semaphore_wait(barrier, len(greeted))
    pair = send(pair_send, pair_recv, p_sem.at[0], p_sem.at[1], partner)
    summary(mine, to_own)

    def link_of(block):
        return jnp.sum(block.astype(F32), axis=0, keepdims=True)

    def spread(logs):
        at = lax.broadcasted_iota(jnp.int32, logs.shape, 1)
        value = jnp.where(at < heads, jnp.exp(logs), 0.0)
        high = value.astype(BF16)
        rest = value - high.astype(F32)
        middle = rest.astype(BF16)
        low = (rest - middle.astype(F32)).astype(BF16)
        hot = e_ref[:, pl.ds(pl.multiple_of(mine, LANE), side_width)]
        return dot(high, hot) + dot(middle, hot) + dot(low, hot)

    pair.wait_recv()
    partner_row = link_of(pair_recv[state:, 0:LANE])
    ll_ref[0:1, :] = jnp.where(is_first, link_row, partner_row)
    ll_ref[1:2, :] = jnp.where(is_first, partner_row, link_row)
    chip_log = link_row + partner_row
    pair_links = spread(ll_ref[0:8, :])
    l0_ref[...] = pair_links[0:1, :]
    tile = link_tile(chip_log, sr)
    for j in range(nz):
        rows = slice(j * sr, (j + 1) * sr)
        own = own_s[rows, :]
        came = pair_recv[rows, :].astype(F32)
        earlier_core = jnp.where(is_first, own, came)
        first_s[rows, :] = earlier_core
        asend[j, :, 0:side_width] = (
            pair_links[1:2, :] * earlier_core + jnp.where(is_first, came, own)
        ).astype(BF16)
        asend[j, :, side_width:] = tile
    sends = [pair]
    row_copies = {}
    for k in around(nz):
        row_copies[k] = send(
            asend.at[(z + k) % nz],
            arecv.at[z],
            a_ssem.at[k - 1],
            a_rsem.at[k - 1],
            in_z[k],
        )
    arecv[z] = asend[z]

    loads[3].wait()
    cj_ref[...] = jnp.where(joined, c_v[...].astype(F32), 0.0).astype(BF16)
    loads[4].wait()

    def alone(first):
        rows = pl.ds(first, step_rows)
        scores = dot_nt(c_v[rows, :], b_v[...])
        at = offset + first + lax.broadcasted_iota(jnp.int32, (step_rows, 1), 0)
        source = offset + lax.broadcasted_iota(jnp.int32, (step_rows, tokens), 1)
        begun = jnp.max(
            jnp.where(starts <= at, starts.astype(F32), -1.0), axis=1, keepdims=True
        )
        live = (source <= at) & (source.astype(F32) >= begun)
        sc_ref[...] = jnp.where(live, scores, 0.0).astype(BF16)
        left = expand(rows, True)
        for cols in columns:
            scale = dot(left, e_ref[:, cols])
            gate = g_v[rows, cols].astype(F32)
            gate = gate / (1.0 + jnp.exp(-gate))
            inside = dot(sc_ref[...], v_ref[:, cols])
            skipped = row_ref[16:17, cols] * x_v[rows, cols].astype(F32)
            a1_ref[rows, cols] = scale * gate
            a2_ref[rows, cols] = (scale * inside + skipped) * gate

    @pl.loop(0, tokens // step_rows)
    def _(i):
        alone(pl.multiple_of(i * step_rows, step_rows))

    for k in around(nz):
        row_copies[k].wait_recv()
    for j in range(nz):
        ll_ref[j : j + 1, :] = link_of(arecv[j, :, side_width:])
    row_log = jnp.sum(ll_ref[0:nz, :], axis=0, keepdims=True)
    lx_ref[0:nz, :] = spread(ll_ref[0:nz, :])
    prefix = jnp.zeros((sr, side_width), F32)
    product = jnp.ones((1, side_width), F32)
    for j in range(nz):
        pre_ref[j] = prefix
        pl_ref[j : j + 1, :] = product
        link = lx_ref[j : j + 1, :]
        prefix = link * prefix + arecv[j, :, 0:side_width].astype(F32)
        product = product * link
    xsend[:, 0:side_width] = prefix.astype(BF16)
    xsend[:, side_width:] = link_tile(row_log, sr)
    x_copies = {}
    for k in around(nx):
        x_copies[k] = send(
            xsend, xrecv.at[xi], x_ssem.at[k - 1], x_rsem.at[k - 1], in_x[k]
        )
    xrecv[xi] = xsend[...]
    for k in around(nx):
        x_copies[k].wait_recv()
    for j in range(nx):
        ll_ref[j : j + 1, :] = link_of(xrecv[j, :, side_width:])
    lx_ref[0:nx, :] = spread(ll_ref[0:nx, :])
    earlier = jnp.zeros((sr, side_width), F32)
    for j in range(nx - 1):
        after = lx_ref[j : j + 1, :] * earlier + xrecv[j, :, 0:side_width].astype(F32)
        earlier = jnp.where(j < xi, after, earlier)
    for j in range(nz):
        bsend[j] = (pre_ref[j] + pl_ref[j : j + 1, :] * earlier).astype(BF16)
    back_copies = {}
    for k in around(nz):
        back_copies[k] = send(
            bsend.at[(z + k) % nz],
            brecv.at[z],
            b_ssem.at[k - 1],
            b_rsem.at[k - 1],
            in_z[k],
        )
    brecv[z] = bsend[z]

    own_lanes = pl.ds(pl.multiple_of(mine, LANE), side_width)
    other_lanes = pl.ds(pl.multiple_of(others, LANE), side_width)
    final_copies = []
    for k in [0] + around(nz)[::-1]:
        if k:
            back_copies[k].wait_recv()
        slot = (z + nz - k) % nz
        rows = pl.ds(pl.multiple_of(slot * sr, sr), sr)
        to_first = brecv[slot].astype(F32)
        to_second = l0_ref[...] * to_first + first_s[rows, :]
        fsend[slot] = jnp.where(is_first, to_second, to_first).astype(BF16)
        final_copies.append(
            send(fsend.at[slot], frecv.at[slot], f_ssem.at[k], f_rsem.at[k], partner)
        )
        sp_ref[rows, own_lanes] = (
            row_ref[8:9, own_lanes] * jnp.where(is_first, to_first, to_second)
        ).astype(BF16)

    sends += [*row_copies.values(), *x_copies.values(), *back_copies.values(), *final_copies]

    def chunk_rows(k):
        return pl.ds(pl.multiple_of(((head + k) % ny) * part, part), part)

    def hidden_columns(rows, cols):
        gated = a2_ref[rows, cols] + a1_ref[rows, cols] * dot(cj_ref[rows, :], sp_ref[:, cols])
        hid_ref[rows, cols] = (gated * gain_ref[cols].reshape(1, cols.size)).astype(BF16)
        return jnp.sum(gated * gated, axis=1, keepdims=True)

    def share_squares(k, squares):
        ss_send[k] = jnp.broadcast_to(as_row(squares, part), (8, part))
        if k:
            return send(
                ss_send.at[k],
                ss_recv.at[k - 1],
                ss_ssem.at[k - 1],
                ss_rsem.at[k - 1],
                in_y[k],
            )

    def make_hidden(k):
        rows = chunk_rows(k)
        squares = jnp.zeros((part, 1), F32)
        for cols in columns:
            squares = squares + hidden_columns(rows, pl.ds(cols.start, 256))
        return share_squares(k, squares)

    def project(k, base, span, store):
        rows = chunk_rows(k)
        for c in range(span[0], span[1], 256):
            store(
                slice(c, c + 256),
                dot(hid_ref[rows, :], w_v[:, base + c : base + c + 256]),
            )

    def into(ref):
        def store(cols, value):
            ref[:, cols] = value.astype(BF16)

        return store

    def added(ref, extra):
        def store(cols, value):
            ref[:, cols] = (value + extra[:, cols].astype(F32)).astype(BF16)

        return store

    far = chunk_rows(2)
    squares = jnp.zeros((part, 1), F32)
    for cut in cuts:
        squares = squares + hidden_columns(far, lanes(mine, cut))
    for copy in final_copies:
        copy.wait_recv()
    for j in range(nz):
        rows = slice(j * sr, (j + 1) * sr)
        sp_ref[rows, other_lanes] = (row_ref[8:9, other_lanes] * frecv[j].astype(F32)).astype(
            BF16
        )
    for cut in cuts:
        squares = squares + hidden_columns(far, lanes(others, cut))
    loads[5].wait()
    up, down = in_y[1], in_y[ny - 1]
    spans = ((0, 512), (512, half))
    first = {}
    for p, span in enumerate(spans):
        for side, device in ((0, up), (1, down)):
            project(2, side * half, span, into(r1_send.at[side]))
            cols = slice(*span)
            first[side, p] = send(
                r1_send.at[side, :, cols],
                r1_recv.at[side, :, cols],
                r1_ssem.at[side, p],
                r1_rsem.at[side, p],
                device,
            )
    squares_sent = [share_squares(2, squares)]
    second = {}
    for side, k, device in ((0, 1, up), (1, ny - 1, down)):
        squares_sent.append(make_hidden(k))
        project(k, (1 - side) * half, (0, half), into(r2_send.at[side, 0]))
        second[side, 0] = send(
            r2_send.at[side, 0],
            r2_recv.at[side, 0],
            r2_ssem.at[side, 0],
            r2_rsem.at[side, 0],
            device,
        )
    make_hidden(0)
    for side in (0, 1):

        def store(cols, value, side=side):
            own_ref[:, side * half + cols.start : side * half + cols.stop] = value

        project(0, side * half, (0, half), store)
    for p, span in enumerate(spans):
        for side, k, device in ((0, 1, up), (1, ny - 1, down)):
            first[side, p].wait_recv()
            project(k, side * half, span, added(r2_send.at[side, 1], r1_recv.at[side]))
            cols = slice(*span)
            second[side, 1 + p] = send(
                r2_send.at[side, 1, :, cols],
                r2_recv.at[side, 1, :, cols],
                r2_ssem.at[side, 1 + p],
                r2_rsem.at[side, 1 + p],
                device,
            )
    for copy in squares_sent:
        copy.wait_recv()
    total_squares = ss_send[0]
    for k in range(ny - 1):
        total_squares = total_squares + ss_recv[k]
    scale = lax.rsqrt(as_column(total_squares[0:1, :], part) / DI + EPSILON)
    for side in (0, 1):
        second[side, 0].wait_recv()
        base = (1 - side) * half
        for c in range(0, half, 256):
            cols = slice(base + c, base + c + 256)
            own_ref[:, cols] = own_ref[:, cols] + r2_recv[side, 0, :, c : c + 256].astype(F32)
    leaving = []
    for p, span in enumerate(spans):
        for side in (0, 1):
            second[side, 1 + p].wait_recv()
            base = side * half
            for c in range(span[0], span[1], 256):
                cols = slice(base + c, base + c + 256)
                value = own_ref[:, cols] + r2_recv[side, 1, :, c : c + 256].astype(F32)
                out_v[:, cols] = (value * scale).astype(BF16)
            cols = slice(base + span[0], base + span[1])
            copy = pltpu.make_async_copy(
                out_v.at[:, cols], out_hbm.at[:, cols], out_sem.at[side, p]
            )
            copy.start()
            leaving.append(copy)
    for copy in sends + squares_sent + [*first.values(), *second.values()]:
        copy.wait_send()
    for copy in leaving:
        copy.wait()


def local(nx, nz, ny, stream, gate, inc, outc, step_raw, bias, rate, skip, gain, proj, starts):
    tokens, channels = stream.shape
    heads = step_raw.shape[0]
    state = inc.shape[1]
    width = proj.shape[1]
    half = width // 2
    sw = channels // 2
    sr = state // nz
    part = tokens // ny
    anyspace = pl.BlockSpec(memory_space=pl.ANY)
    vmem = pl.BlockSpec(memory_space=pltpu.VMEM)
    dma = pltpu.SemaphoreType.DMA
    scratch = [
        pltpu.VMEM((tokens, channels), BF16),
        pltpu.VMEM((tokens, channels), BF16),
        pltpu.VMEM((tokens, state), BF16),
        pltpu.VMEM((tokens, state), BF16),
        pltpu.VMEM((heads, tokens), F32),
        pltpu.VMEM((channels, width), BF16),
        pltpu.VMEM((LANE, tokens + LANE), F32),
        pltpu.VMEM((tokens + LANE, LANE), BF16),
        pltpu.VMEM((LANE, channels), BF16),
        pltpu.VMEM((tokens, channels), BF16),
        pltpu.VMEM((128, tokens), BF16),
        pltpu.VMEM((tokens, state), BF16),
        pltpu.VMEM((tokens, channels), F32),
        pltpu.VMEM((tokens, channels), F32),
        pltpu.VMEM((24, channels), F32),
        pltpu.VMEM((state, sw), F32),
        pltpu.VMEM((state + 8, sw), BF16),
        pltpu.VMEM((state + 8, sw), BF16),
        pltpu.VMEM((state, sw), F32),
        pltpu.VMEM((nz, sr, sw + LANE), BF16),
        pltpu.VMEM((nz, sr, sw + LANE), BF16),
        pltpu.VMEM((8, LANE), F32),
        pltpu.VMEM((8, sw), F32),
        pltpu.VMEM((1, sw), F32),
        pltpu.VMEM((nz, sr, sw), F32),
        pltpu.VMEM((8, sw), F32),
        pltpu.VMEM((sr, sw + LANE), BF16),
        pltpu.VMEM((nx, sr, sw + LANE), BF16),
        pltpu.VMEM((nz, sr, sw), BF16),
        pltpu.VMEM((nz, sr, sw), BF16),
        pltpu.VMEM((nz, sr, sw), BF16),
        pltpu.VMEM((nz, sr, sw), BF16),
        pltpu.VMEM((state, channels), BF16),
        pltpu.VMEM((tokens, channels), BF16),
        pltpu.VMEM((2, part, half), BF16),
        pltpu.VMEM((2, part, half), BF16),
        pltpu.VMEM((2, 2, part, half), BF16),
        pltpu.VMEM((2, 2, part, half), BF16),
        pltpu.VMEM((part, width), F32),
        pltpu.VMEM((part, width), BF16),
        pltpu.VMEM((ny, 8, part), F32),
        pltpu.VMEM((ny - 1, 8, part), F32),
        dma((6,)),
        dma((2,)),
        dma((nz - 1,)),
        dma((nz - 1,)),
        dma((nx - 1,)),
        dma((nx - 1,)),
        dma((nz - 1,)),
        dma((nz - 1,)),
        dma((nz,)),
        dma((nz,)),
        dma((2, 2)),
        dma((2, 2)),
        dma((2, 3)),
        dma((2, 3)),
        dma((ny - 1,)),
        dma((ny - 1,)),
        dma((2, 2)),
    ]
    return pl.pallas_call(
        functools.partial(kernel, nx, nz, ny),
        out_shape=jax.ShapeDtypeStruct((part, width), BF16),
        in_specs=[anyspace] * 5 + [vmem] * 4 + [anyspace, vmem],
        out_specs=anyspace,
        scratch_shapes=scratch,
        compiler_params=pltpu.CompilerParams(
            collective_id=0, has_side_effects=True, vmem_limit_bytes=56 * 1024 * 1024
        ),
        name="ssd_layer",
    )(
        stream,
        gate,
        inc,
        outc,
        step_raw,
        bias[None],
        rate[None],
        skip[None],
        gain,
        proj,
        starts[None],
    )


def solution(mesh):
    chips = mesh.shape["seq"] // 2
    nz = min(ALONG_Z, chips)
    in_specs = (
        P("seq", "head"),
        P("seq", "head"),
        P("seq", None),
        P("seq", None),
        P("head", "seq"),
        P("head"),
        P("head"),
        P("head"),
        P("head"),
        P("head", None),
        P(),
    )
    return jax.shard_map(
        functools.partial(local, chips // nz, nz, mesh.shape["head"]),
        mesh=mesh,
        in_specs=in_specs,
        out_specs=P(("seq", "head"), None),
        check_vma=False,
    )
```

time: 63.9 us -> 58.2 us (0.911)
  Pallas kernels: 60.4 us -> 56.1 us
  local copies, waits for them, and re-layouts: 3.26 us -> 1.97 us
    pallas_call x1, Pallas kernels: 60.4 us -> 56.1 us  [local(): pl.pallas_call(functools.partial(kernel, nx, nz, ny), out_shape=jax.Shape...]
    broadcast_in_dim x1 -> x0, local copies, waits for them, and re-layouts: 1.29 us -> none  [local(): gain[None]]
where the time goes in v2:
time: 58.2 us; the launch traced here: 58.1 us
  Pallas kernels  56.1 us (96%)
  local copies, waits for them, and re-layouts  1.97 us (3%)
    pallas_call x1, Pallas kernels, local(): pl.pallas_call(functools.partial(kernel, nx, nz, ny), out_shape=jax.Shape...  56.1 us
    unnamed x1, local copies, waits for them, and re-layouts  1.97 us

profile of v2, /device:TPU:1, one launch (start us, length us, event | category | flops | bytes accessed | tf_op | source)
XLA Modules:
  0.0 58.1 jit_solution(583639602315370398)
XLA Ops:
  0.0 56.1 %ssd_layer.1 = bf16[128,2560]{1,0:T(8,128)(2,1)} custom-call(bf16[512,1280]{1,0:T(8,128)(2,1)} %x_hbm.1, bf16[512,1280]{1,0:T(8,128)(2,1)} %g_hbm.1, bf16[512,128]{1,0:T(8,128)(2,1)} %b_hbm.1, bf16[512,128]{1,0:T(8,128)(2,1)} %c_hbm.1, f32[20,512]{1,0:T(8,128)} %st_hbm.1, f32[1,20]{1,0:T(1,128)} %bitcast.4, f32[1,20]{1,0:T(1,128)} %bitcast.5, ...), custom_call_target="tpu_custom_call" | custom-call | tf_op jit(solution)/shard_map/ssd_layer/pallas_call | solution.py:646
  56.1 2.0 %copy.13 = bf16[128,2560]{1,0:T(8,128)(2,1)} copy(bf16[128,2560]{1,0:T(8,128)(2,1)} %ssd_layer.1) | data formatting | bytes 1310720

commit v3 on v2

--- a/solution.py
+++ b/solution.py
@@ -59,13 +59,18 @@
     b_hbm,
     c_hbm,
     st_hbm,
+    bias_hbm,
+    rate_hbm,
+    skip_hbm,
+    gain_hbm,
+    w_hbm,
+    doc_hbm,
+    out_hbm,
     bias_ref,
     rate_ref,
     skip_ref,
     gain_ref,
-    w_hbm,
     doc_ref,
-    out_hbm,
     x_v,
     g_v,
     b_v,
@@ -87,6 +92,10 @@
     first_s,
     asend,
     arecv,
+    zlog_send,
+    zlog_recv,
+    xlog_send,
+    xlog_recv,
     ll_ref,
     lx_ref,
     l0_ref,
@@ -108,8 +117,13 @@
     out_v,
     ss_send,
     ss_recv,
+    small_sem,
     copy_sem,
     p_sem,
+    la_ssem,
+    la_rsem,
+    lx_ssem,
+    lx_rsem,
     a_ssem,
     a_rsem,
     x_ssem,
@@ -143,6 +157,27 @@
     offset = seq * tokens
     head_size = channels // heads
 
+    barrier = pltpu.get_barrier_semaphore()
+    partner = (seq + 1 - 2 * core, head)
+    in_z = [((xi * nz + (z + k) % nz) * 2 + core, head) for k in range(nz)]
+    in_x = [((((xi + k) % nx) * nz + z) * 2 + core, head) for k in range(nx)]
+    in_y = [(seq, (head + k) % ny) for k in range(ny)]
+    greeted = in_z[1:] + in_x[1:] + in_y[1:] + [partner]
+    for device in greeted:
+        pl.semaphore_signal(barrier, inc=1, device_id=device, device_id_type=MESH)
+
+    small = [
+        pltpu.make_async_copy(src, dst, small_sem.at[i])
+        for i, (src, dst) in enumerate(
+            (
+                (doc_hbm, doc_ref),
+                (bias_hbm, bias_ref),
+                (rate_hbm, rate_ref),
+                (skip_hbm, skip_ref),
+                (gain_hbm, gain_ref),
+            )
+        )
+    ]
     loads = [
         pltpu.make_async_copy(src, dst, copy_sem.at[i])
         for i, (src, dst) in enumerate(
@@ -156,17 +191,8 @@
             )
         )
     ]
-    for load in loads[:3]:
+    for load in [loads[0], *small, *loads[1:3]]:
         load.start()
-
-    barrier = pltpu.get_barrier_semaphore()
-    partner = (seq + 1 - 2 * core, head)
-    in_z = [((xi * nz + (z + k) % nz) * 2 + core, head) for k in range(nz)]
-    in_x = [((((xi + k) % nx) * nz + z) * 2 + core, head) for k in range(nx)]
-    in_y = [(seq, (head + k) % ny) for k in range(ny)]
-    greeted = in_z[1:] + in_x[1:] + in_y[1:] + [partner]
-    for device in greeted:
-        pl.semaphore_signal(barrier, inc=1, device_id=device, device_id_type=MESH)
 
     def send(src, dst, ssem, rsem, device):
         copy = pltpu.make_async_remote_copy(
@@ -192,6 +218,7 @@
     ).astype(F32).astype(BF16)
     m_ref[...] = jnp.zeros_like(m_ref)
     ll_ref[...] = jnp.zeros_like(ll_ref)
+    small[0].wait()
     starts = doc_ref[...]
     position = offset + lax.broadcasted_iota(jnp.int32, (tokens, 1), 0)
     doc_start = jnp.max(
@@ -200,6 +227,8 @@
     joined = doc_start < offset.astype(F32)
     last_start = doc_start[tokens - 1 :, :]
 
+    for load in small[1:]:
+        load.wait()
     bias = as_column(bias_ref[...], heads)
     rate = as_column(rate_ref[...], heads)
     skip = as_column(skip_ref[...], heads)
@@ -317,18 +346,23 @@
     chip_log = link_row + partner_row
     pair_links = spread(ll_ref[0:8, :])
     l0_ref[...] = pair_links[0:1, :]
-    tile = link_tile(chip_log, sr)
+    sends = [pair]
+    zlog_send[...] = chip_log
+    zlog_copies = {}
+    for k in around(nz):
+        zlog_copies[k] = send(
+            zlog_send, zlog_recv.at[z], la_ssem.at[k - 1], la_rsem.at[k - 1], in_z[k]
+        )
+    zlog_recv[z] = chip_log
     for j in range(nz):
         rows = slice(j * sr, (j + 1) * sr)
         own = own_s[rows, :]
         came = pair_recv[rows, :].astype(F32)
         earlier_core = jnp.where(is_first, own, came)
         first_s[rows, :] = earlier_core
-        asend[j, :, 0:side_width] = (
+        asend[j] = (
             pair_links[1:2, :] * earlier_core + jnp.where(is_first, came, own)
         ).astype(BF16)
-        asend[j, :, side_width:] = tile
-    sends = [pair]
     row_copies = {}
     for k in around(nz):
         row_copies[k] = send(
@@ -369,21 +403,29 @@
         alone(pl.multiple_of(i * step_rows, step_rows))
 
     for k in around(nz):
+        zlog_copies[k].wait_recv()
+    for j in range(nz):
+        ll_ref[j : j + 1, :] = zlog_recv[j]
+    row_log = jnp.sum(ll_ref[0:nz, :], axis=0, keepdims=True)
+    xlog_send[...] = row_log
+    xlog_copies = {}
+    for k in around(nx):
+        xlog_copies[k] = send(
+            xlog_send, xlog_recv.at[xi], lx_ssem.at[k - 1], lx_rsem.at[k - 1], in_x[k]
+        )
+    xlog_recv[xi] = row_log
+    lx_ref[0:nz, :] = spread(ll_ref[0:nz, :])
+    for k in around(nz):
         row_copies[k].wait_recv()
-    for j in range(nz):
-        ll_ref[j : j + 1, :] = link_of(arecv[j, :, side_width:])
-    row_log = jnp.sum(ll_ref[0:nz, :], axis=0, keepdims=True)
-    lx_ref[0:nz, :] = spread(ll_ref[0:nz, :])
     prefix = jnp.zeros((sr, side_width), F32)
     product = jnp.ones((1, side_width), F32)
     for j in range(nz):
         pre_ref[j] = prefix
         pl_ref[j : j + 1, :] = product
         link = lx_ref[j : j + 1, :]
-        prefix = link * prefix + arecv[j, :, 0:side_width].astype(F32)
+        prefix = link * prefix + arecv[j].astype(F32)
         product = product * link
-    xsend[:, 0:side_width] = prefix.astype(BF16)
-    xsend[:, side_width:] = link_tile(row_log, sr)
+    xsend[...] = prefix.astype(BF16)
     x_copies = {}
     for k in around(nx):
         x_copies[k] = send(
@@ -391,13 +433,15 @@
         )
     xrecv[xi] = xsend[...]
     for k in around(nx):
+        xlog_copies[k].wait_recv()
+    for j in range(nx):
+        ll_ref[j : j + 1, :] = xlog_recv[j]
+    lx_ref[0:nx, :] = spread(ll_ref[0:nx, :])
+    for k in around(nx):
         x_copies[k].wait_recv()
-    for j in range(nx):
-        ll_ref[j : j + 1, :] = link_of(xrecv[j, :, side_width:])
-    lx_ref[0:nx, :] = spread(ll_ref[0:nx, :])
     earlier = jnp.zeros((sr, side_width), F32)
     for j in range(nx - 1):
-        after = lx_ref[j : j + 1, :] * earlier + xrecv[j, :, 0:side_width].astype(F32)
+        after = lx_ref[j : j + 1, :] * earlier + xrecv[j].astype(F32)
         earlier = jnp.where(j < xi, after, earlier)
     for j in range(nz):
         bsend[j] = (pre_ref[j] + pl_ref[j : j + 1, :] * earlier).astype(BF16)
@@ -430,7 +474,9 @@
             row_ref[8:9, own_lanes] * jnp.where(is_first, to_first, to_second)
         ).astype(BF16)
 
-    sends += [*row_copies.values(), *x_copies.values(), *back_copies.values(), *final_copies]
+    for copies in (zlog_copies, row_copies, xlog_copies, x_copies, back_copies):
+        sends += copies.values()
+    sends += final_copies
 
     def chunk_rows(k):
         return pl.ds(pl.multiple_of(((head + k) % ny) * part, part), part)
@@ -493,7 +539,8 @@
         squares = squares + hidden_columns(far, lanes(others, cut))
     loads[5].wait()
     up, down = in_y[1], in_y[ny - 1]
-    spans = ((0, 512), (512, half))
+    spans = ((0, 256), (256, half))
+    last_spans = ((0, half - 256), (half - 256, half))
     first = {}
     for p, span in enumerate(spans):
         for side, device in ((0, up), (1, down)):
@@ -525,9 +572,11 @@
             own_ref[:, side * half + cols.start : side * half + cols.stop] = value
 
         project(0, side * half, (0, half), store)
-    for p, span in enumerate(spans):
+    for p, span in enumerate(last_spans):
         for side, k, device in ((0, 1, up), (1, ny - 1, down)):
-            first[side, p].wait_recv()
+            if p == 0:
+                first[side, 0].wait_recv()
+                first[side, 1].wait_recv()
             project(k, side * half, span, added(r2_send.at[side, 1], r1_recv.at[side]))
             cols = slice(*span)
             second[side, 1 + p] = send(
@@ -550,7 +599,7 @@
             cols = slice(base + c, base + c + 256)
             own_ref[:, cols] = own_ref[:, cols] + r2_recv[side, 0, :, c : c + 256].astype(F32)
     leaving = []
-    for p, span in enumerate(spans):
+    for p, span in enumerate(last_spans):
         for side in (0, 1):
             second[side, 1 + p].wait_recv()
             base = side * half
@@ -580,9 +629,13 @@
     sr = state // nz
     part = tokens // ny
     anyspace = pl.BlockSpec(memory_space=pl.ANY)
-    vmem = pl.BlockSpec(memory_space=pltpu.VMEM)
     dma = pltpu.SemaphoreType.DMA
     scratch = [
+        pltpu.VMEM((1, heads), F32),
+        pltpu.VMEM((1, heads), F32),
+        pltpu.VMEM((1, heads), F32),
+        pltpu.VMEM((channels,), F32),
+        pltpu.VMEM((1, starts.shape[0]), jnp.int32),
         pltpu.VMEM((tokens, channels), BF16),
         pltpu.VMEM((tokens, channels), BF16),
         pltpu.VMEM((tokens, state), BF16),
@@ -602,15 +655,19 @@
         pltpu.VMEM((state + 8, sw), BF16),
         pltpu.VMEM((state + 8, sw), BF16),
         pltpu.VMEM((state, sw), F32),
-        pltpu.VMEM((nz, sr, sw + LANE), BF16),
-        pltpu.VMEM((nz, sr, sw + LANE), BF16),
+        pltpu.VMEM((nz, sr, sw), BF16),
+        pltpu.VMEM((nz, sr, sw), BF16),
+        pltpu.VMEM((1, LANE), F32),
+        pltpu.VMEM((nz, 1, LANE), F32),
+        pltpu.VMEM((1, LANE), F32),
+        pltpu.VMEM((nx, 1, LANE), F32),
         pltpu.VMEM((8, LANE), F32),
         pltpu.VMEM((8, sw), F32),
         pltpu.VMEM((1, sw), F32),
         pltpu.VMEM((nz, sr, sw), F32),
         pltpu.VMEM((8, sw), F32),
-        pltpu.VMEM((sr, sw + LANE), BF16),
-        pltpu.VMEM((nx, sr, sw + LANE), BF16),
+        pltpu.VMEM((sr, sw), BF16),
+        pltpu.VMEM((nx, sr, sw), BF16),
         pltpu.VMEM((nz, sr, sw), BF16),
         pltpu.VMEM((nz, sr, sw), BF16),
         pltpu.VMEM((nz, sr, sw), BF16),
@@ -625,8 +682,13 @@
         pltpu.VMEM((part, width), BF16),
         pltpu.VMEM((ny, 8, part), F32),
         pltpu.VMEM((ny - 1, 8, part), F32),
+        dma((5,)),
         dma((6,)),
         dma((2,)),
+        dma((nz - 1,)),
+        dma((nz - 1,)),
+        dma((nx - 1,)),
+        dma((nx - 1,)),
         dma((nz - 1,)),
         dma((nz - 1,)),
         dma((nx - 1,)),
@@ -646,7 +708,7 @@
     return pl.pallas_call(
         functools.partial(kernel, nx, nz, ny),
         out_shape=jax.ShapeDtypeStruct((part, width), BF16),
-        in_specs=[anyspace] * 5 + [vmem] * 4 + [anyspace, vmem],
+        in_specs=[anyspace] * 11,
         out_specs=anyspace,
         scratch_shapes=scratch,
         compiler_params=pltpu.CompilerParams(

time: 58.2 us -> 56.6 us (0.973)
  Pallas kernels: 56.1 us -> 54.5 us
    pallas_call x1, Pallas kernels: 56.1 us -> 54.5 us  [local(): pl.pallas_call(functools.partial(kernel, nx, nz, ny), out_shape=jax.Shape...]
where the time goes in v3:
time: 56.6 us; the launch traced here: 56.5 us
  Pallas kernels  54.5 us (96%)
  local copies, waits for them, and re-layouts  1.97 us (3%)
    pallas_call x1, Pallas kernels, local(): pl.pallas_call(functools.partial(kernel, nx, nz, ny), out_shape=jax.Shape...  54.5 us
    unnamed x1, local copies, waits for them, and re-layouts  1.97 us

profile of v3, /device:TPU:1, one launch (start us, length us, event | category | flops | bytes accessed | tf_op | source)
XLA Modules:
  0.0 56.5 jit_solution(1918486594658585686)
XLA Ops:
  0.0 54.5 %ssd_layer.1 = bf16[128,2560]{1,0:T(8,128)(2,1)} custom-call(bf16[512,1280]{1,0:T(8,128)(2,1)} %x_hbm.1, bf16[512,1280]{1,0:T(8,128)(2,1)} %g_hbm.1, bf16[512,128]{1,0:T(8,128)(2,1)} %b_hbm.1, bf16[512,128]{1,0:T(8,128)(2,1)} %c_hbm.1, f32[20,512]{1,0:T(8,128)} %st_hbm.1, f32[1,20]{1,0:T(1,128)} %bitcast.4, f32[1,20]{1,0:T(1,128)} %bitcast.5, ...), custom_call_target="tpu_custom_call" | custom-call | tf_op jit(solution)/shard_map/ssd_layer/pallas_call | solution.py:708
  54.5 2.0 %copy.13 = bf16[128,2560]{1,0:T(8,128)(2,1)} copy(bf16[128,2560]{1,0:T(8,128)(2,1)} %ssd_layer.1) | data formatting | bytes 1310720

commit v4 on v3

--- a/solution.py
+++ b/solution.py
@@ -65,7 +65,7 @@
     gain_hbm,
     w_hbm,
     doc_hbm,
-    out_hbm,
+    out_ref,
     bias_ref,
     rate_ref,
     skip_ref,
@@ -114,7 +114,6 @@
     r2_send,
     r2_recv,
     own_ref,
-    out_v,
     ss_send,
     ss_recv,
     small_sem,
@@ -138,7 +137,6 @@
     r2_rsem,
     ss_ssem,
     ss_rsem,
-    out_sem,
 ):
     seq = lax.axis_index("seq")
     head = lax.axis_index("head")
@@ -346,7 +344,6 @@
     chip_log = link_row + partner_row
     pair_links = spread(ll_ref[0:8, :])
     l0_ref[...] = pair_links[0:1, :]
-    sends = [pair]
     zlog_send[...] = chip_log
     zlog_copies = {}
     for k in around(nz):
@@ -354,25 +351,22 @@
             zlog_send, zlog_recv.at[z], la_ssem.at[k - 1], la_rsem.at[k - 1], in_z[k]
         )
     zlog_recv[z] = chip_log
-    for j in range(nz):
-        rows = slice(j * sr, (j + 1) * sr)
+    row_copies = {}
+    for k in [*around(nz), 0]:
+        slot = (z + k) % nz
+        rows = pl.ds(pl.multiple_of(slot * sr, sr), sr)
         own = own_s[rows, :]
         came = pair_recv[rows, :].astype(F32)
         earlier_core = jnp.where(is_first, own, came)
         first_s[rows, :] = earlier_core
-        asend[j] = (
-            pair_links[1:2, :] * earlier_core + jnp.where(is_first, came, own)
-        ).astype(BF16)
-    row_copies = {}
-    for k in around(nz):
-        row_copies[k] = send(
-            asend.at[(z + k) % nz],
-            arecv.at[z],
-            a_ssem.at[k - 1],
-            a_rsem.at[k - 1],
-            in_z[k],
-        )
-    arecv[z] = asend[z]
+        merged = pair_links[1:2, :] * earlier_core + jnp.where(is_first, came, own)
+        if k:
+            asend[slot] = merged.astype(BF16)
+            row_copies[k] = send(
+                asend.at[slot], arecv.at[z], a_ssem.at[k - 1], a_rsem.at[k - 1], in_z[k]
+            )
+        else:
+            arecv[z] = merged.astype(BF16)
 
     loads[3].wait()
     cj_ref[...] = jnp.where(joined, c_v[...].astype(F32), 0.0).astype(BF16)
@@ -443,18 +437,17 @@
     for j in range(nx - 1):
         after = lx_ref[j : j + 1, :] * earlier + xrecv[j].astype(F32)
         earlier = jnp.where(j < xi, after, earlier)
-    for j in range(nz):
-        bsend[j] = (pre_ref[j] + pl_ref[j : j + 1, :] * earlier).astype(BF16)
     back_copies = {}
-    for k in around(nz):
-        back_copies[k] = send(
-            bsend.at[(z + k) % nz],
-            brecv.at[z],
-            b_ssem.at[k - 1],
-            b_rsem.at[k - 1],
-            in_z[k],
-        )
-    brecv[z] = bsend[z]
+    for k in [*around(nz), 0]:
+        slot = (z + k) % nz
+        value = (pre_ref[slot] + pl_ref[pl.ds(slot, 1), :] * earlier).astype(BF16)
+        if k:
+            bsend[slot] = value
+            back_copies[k] = send(
+                bsend.at[slot], brecv.at[z], b_ssem.at[k - 1], b_rsem.at[k - 1], in_z[k]
+            )
+        else:
+            brecv[z] = value
 
     own_lanes = pl.ds(pl.multiple_of(mine, LANE), side_width)
     other_lanes = pl.ds(pl.multiple_of(others, LANE), side_width)
@@ -474,6 +467,7 @@
             row_ref[8:9, own_lanes] * jnp.where(is_first, to_first, to_second)
         ).astype(BF16)
 
+    sends = [pair]
     for copies in (zlog_copies, row_copies, xlog_copies, x_copies, back_copies):
         sends += copies.values()
     sends += final_copies
@@ -598,7 +592,6 @@
         for c in range(0, half, 256):
             cols = slice(base + c, base + c + 256)
             own_ref[:, cols] = own_ref[:, cols] + r2_recv[side, 0, :, c : c + 256].astype(F32)
-    leaving = []
     for p, span in enumerate(last_spans):
         for side in (0, 1):
             second[side, 1 + p].wait_recv()
@@ -606,17 +599,9 @@
             for c in range(span[0], span[1], 256):
                 cols = slice(base + c, base + c + 256)
                 value = own_ref[:, cols] + r2_recv[side, 1, :, c : c + 256].astype(F32)
-                out_v[:, cols] = (value * scale).astype(BF16)
-            cols = slice(base + span[0], base + span[1])
-            copy = pltpu.make_async_copy(
-                out_v.at[:, cols], out_hbm.at[:, cols], out_sem.at[side, p]
-            )
-            copy.start()
-            leaving.append(copy)
+                out_ref[:, cols] = (value * scale).astype(BF16)
     for copy in sends + squares_sent + [*first.values(), *second.values()]:
         copy.wait_send()
-    for copy in leaving:
-        copy.wait()
 
 
 def local(nx, nz, ny, stream, gate, inc, outc, step_raw, bias, rate, skip, gain, proj, starts):
@@ -679,7 +664,6 @@
         pltpu.VMEM((2, 2, part, half), BF16),
         pltpu.VMEM((2, 2, part, half), BF16),
         pltpu.VMEM((part, width), F32),
-        pltpu.VMEM((part, width), BF16),
         pltpu.VMEM((ny, 8, part), F32),
         pltpu.VMEM((ny - 1, 8, part), F32),
         dma((5,)),
@@ -703,13 +687,12 @@
         dma((2, 3)),
         dma((ny - 1,)),
         dma((ny - 1,)),
-        dma((2, 2)),
     ]
     return pl.pallas_call(
         functools.partial(kernel, nx, nz, ny),
-        out_shape=jax.ShapeDtypeStruct((part, width), BF16),
+        out_shape=pltpu.VMEM((part, width), BF16),
         in_specs=[anyspace] * 11,
-        out_specs=anyspace,
+        out_specs=pl.BlockSpec(memory_space=pltpu.VMEM),
         scratch_shapes=scratch,
         compiler_params=pltpu.CompilerParams(
             collective_id=0, has_side_effects=True, vmem_limit_bytes=56 * 1024 * 1024

time: 56.6 us -> 54.8 us (0.968)
  local copies, waits for them, and re-layouts: 1.97 us -> 0.84 us
  Pallas kernels: 54.5 us -> 53.9 us
    unnamed x1, local copies, waits for them, and re-layouts: 1.97 us -> 0.84 us
    pallas_call x1, Pallas kernels: 54.5 us -> 53.9 us  [local(): pl.pallas_call(functools.partial(kernel, nx, nz, ny), out_shape=pltpu.VME...]
where the time goes in v4:
time: 54.8 us; the launch traced here: 54.7 us
  Pallas kernels  53.9 us (98%)
  local copies, waits for them, and re-layouts  0.84 us (2%)
    pallas_call x1, Pallas kernels, local(): pl.pallas_call(functools.partial(kernel, nx, nz, ny), out_shape=pltpu.VME...  53.9 us

profile of v4, /device:TPU:1, one launch (start us, length us, event | category | flops | bytes accessed | tf_op | source)
XLA Modules:
  0.0 54.7 jit_solution(1156076294685491019)
XLA Ops:
  0.0 53.9 %ssd_layer.1 = bf16[128,2560]{1,0:T(8,128)(2,1)S(1)} custom-call(bf16[512,1280]{1,0:T(8,128)(2,1)} %x_hbm.1, bf16[512,1280]{1,0:T(8,128)(2,1)} %g_hbm.1, bf16[512,128]{1,0:T(8,128)(2,1)} %b_hbm.1, bf16[512,128]{1,0:T(8,128)(2,1)} %c_hbm.1, f32[20,512]{1,0:T(8,128)} %st_hbm.1, f32[1,20]{1,0:T(1,128)} %bitcast.4, f32[1,20]{1,0:T(1,128)} %bitcast.5, ...), custom_call_target="tpu_custom_call" | custom-call | tf_op jit(solution)/shard_map/ssd_layer/pallas_call | solution.py:691
  53.9 0.8 %copy.13 = bf16[128,2560]{1,0:T(8,128)(2,1)} copy(bf16[128,2560]{1,0:T(8,128)(2,1)S(1)} %ssd_layer.1) | data formatting | bytes 1310720

commit v5 on v4

--- a/solution.py
+++ b/solution.py
@@ -352,6 +352,18 @@
         )
     zlog_recv[z] = chip_log
     row_copies = {}
+    cut_at = (side_width * 3 // 5) // LANE * LANE
+    groups = (slice(0, cut_at), slice(cut_at, side_width))
+
+    def send_out(g, k, slot):
+        row_copies[g, k] = send(
+            asend.at[slot, :, groups[g]],
+            arecv.at[z, :, groups[g]],
+            a_ssem.at[g, k - 1],
+            a_rsem.at[g, k - 1],
+            in_z[k],
+        )
+
     for k in [*around(nz), 0]:
         slot = (z + k) % nz
         rows = pl.ds(pl.multiple_of(slot * sr, sr), sr)
@@ -362,11 +374,11 @@
         merged = pair_links[1:2, :] * earlier_core + jnp.where(is_first, came, own)
         if k:
             asend[slot] = merged.astype(BF16)
-            row_copies[k] = send(
-                asend.at[slot], arecv.at[z], a_ssem.at[k - 1], a_rsem.at[k - 1], in_z[k]
-            )
+            send_out(0, k, slot)
         else:
             arecv[z] = merged.astype(BF16)
+    for k in around(nz):
+        send_out(1, k, (z + k) % nz)
 
     loads[3].wait()
     cj_ref[...] = jnp.where(joined, c_v[...].astype(F32), 0.0).astype(BF16)
@@ -409,63 +421,80 @@
         )
     xlog_recv[xi] = row_log
     lx_ref[0:nz, :] = spread(ll_ref[0:nz, :])
-    for k in around(nz):
-        row_copies[k].wait_recv()
-    prefix = jnp.zeros((sr, side_width), F32)
-    product = jnp.ones((1, side_width), F32)
-    for j in range(nz):
-        pre_ref[j] = prefix
-        pl_ref[j : j + 1, :] = product
-        link = lx_ref[j : j + 1, :]
-        prefix = link * prefix + arecv[j].astype(F32)
-        product = product * link
-    xsend[...] = prefix.astype(BF16)
     x_copies = {}
-    for k in around(nx):
-        x_copies[k] = send(
-            xsend, xrecv.at[xi], x_ssem.at[k - 1], x_rsem.at[k - 1], in_x[k]
-        )
-    xrecv[xi] = xsend[...]
+    for g, cols in enumerate(groups):
+        for k in around(nz):
+            row_copies[g, k].wait_recv()
+        prefix = jnp.zeros((sr, cols.stop - cols.start), F32)
+        product = jnp.ones((1, cols.stop - cols.start), F32)
+        for j in range(nz):
+            pre_ref[j, :, cols] = prefix
+            pl_ref[j : j + 1, cols] = product
+            link = lx_ref[j : j + 1, cols]
+            prefix = link * prefix + arecv[j, :, cols].astype(F32)
+            product = product * link
+        xsend[:, cols] = prefix.astype(BF16)
+        for k in around(nx):
+            x_copies[g, k] = send(
+                xsend.at[:, cols],
+                xrecv.at[xi, :, cols],
+                x_ssem.at[g, k - 1],
+                x_rsem.at[g, k - 1],
+                in_x[k],
+            )
+        xrecv[xi, :, cols] = xsend[:, cols]
     for k in around(nx):
         xlog_copies[k].wait_recv()
     for j in range(nx):
         ll_ref[j : j + 1, :] = xlog_recv[j]
     lx_ref[0:nx, :] = spread(ll_ref[0:nx, :])
-    for k in around(nx):
-        x_copies[k].wait_recv()
-    earlier = jnp.zeros((sr, side_width), F32)
-    for j in range(nx - 1):
-        after = lx_ref[j : j + 1, :] * earlier + xrecv[j].astype(F32)
-        earlier = jnp.where(j < xi, after, earlier)
     back_copies = {}
-    for k in [*around(nz), 0]:
-        slot = (z + k) % nz
-        value = (pre_ref[slot] + pl_ref[pl.ds(slot, 1), :] * earlier).astype(BF16)
-        if k:
-            bsend[slot] = value
-            back_copies[k] = send(
-                bsend.at[slot], brecv.at[z], b_ssem.at[k - 1], b_rsem.at[k - 1], in_z[k]
-            )
-        else:
-            brecv[z] = value
-
-    own_lanes = pl.ds(pl.multiple_of(mine, LANE), side_width)
+    for g, cols in enumerate(groups):
+        for k in around(nx):
+            x_copies[g, k].wait_recv()
+        earlier = jnp.zeros((sr, cols.stop - cols.start), F32)
+        for j in range(nx - 1):
+            after = lx_ref[j : j + 1, cols] * earlier + xrecv[j, :, cols].astype(F32)
+            earlier = jnp.where(j < xi, after, earlier)
+        for k in [*around(nz), 0]:
+            slot = (z + k) % nz
+            value = (pre_ref[slot, :, cols] + pl_ref[pl.ds(slot, 1), cols] * earlier).astype(BF16)
+            if k:
+                bsend[slot, :, cols] = value
+                back_copies[g, k] = send(
+                    bsend.at[slot, :, cols],
+                    brecv.at[z, :, cols],
+                    b_ssem.at[g, k - 1],
+                    b_rsem.at[g, k - 1],
+                    in_z[k],
+                )
+            else:
+                brecv[z, :, cols] = value
+
     other_lanes = pl.ds(pl.multiple_of(others, LANE), side_width)
     final_copies = []
-    for k in [0] + around(nz)[::-1]:
-        if k:
-            back_copies[k].wait_recv()
-        slot = (z + nz - k) % nz
-        rows = pl.ds(pl.multiple_of(slot * sr, sr), sr)
-        to_first = brecv[slot].astype(F32)
-        to_second = l0_ref[...] * to_first + first_s[rows, :]
-        fsend[slot] = jnp.where(is_first, to_second, to_first).astype(BF16)
-        final_copies.append(
-            send(fsend.at[slot], frecv.at[slot], f_ssem.at[k], f_rsem.at[k], partner)
-        )
-        sp_ref[rows, own_lanes] = (
-            row_ref[8:9, own_lanes] * jnp.where(is_first, to_first, to_second)
-        ).astype(BF16)
+    for g, cols in enumerate(groups):
+        own_lanes = pl.ds(pl.multiple_of(mine + cols.start, LANE), cols.stop - cols.start)
+        for k in [0] + around(nz)[::-1]:
+            if k:
+                back_copies[g, k].wait_recv()
+            slot = (z + nz - k) % nz
+            rows = pl.ds(pl.multiple_of(slot * sr, sr), sr)
+            to_first = brecv[slot, :, cols].astype(F32)
+            to_second = l0_ref[:, cols] * to_first + first_s[rows, cols]
+            fsend[slot, :, cols] = jnp.where(is_first, to_second, to_first).astype(BF16)
+            final_copies.append(
+                send(
+                    fsend.at[slot, :, cols],
+                    frecv.at[slot, :, cols],
+                    f_ssem.at[g, k],
+                    f_rsem.at[g, k],
+                    partner,
+                )
+            )
+            sp_ref[rows, own_lanes] = (
+                row_ref[8:9, own_lanes] * jnp.where(is_first, to_first, to_second)
+            ).astype(BF16)
 
     sends = [pair]
     for copies in (zlog_copies, row_copies, xlog_copies, x_copies, back_copies):
@@ -673,14 +702,14 @@
         dma((nz - 1,)),
         dma((nx - 1,)),
         dma((nx - 1,)),
-        dma((nz - 1,)),
-        dma((nz - 1,)),
-        dma((nx - 1,)),
-        dma((nx - 1,)),
-        dma((nz - 1,)),
-        dma((nz - 1,)),
-        dma((nz,)),
-        dma((nz,)),
+        dma((2, nz - 1)),
+        dma((2, nz - 1)),
+        dma((2, nx - 1)),
+        dma((2, nx - 1)),
+        dma((2, nz - 1)),
+        dma((2, nz - 1)),
+        dma((2, nz)),
+        dma((2, nz)),
         dma((2, 2)),
         dma((2, 2)),
         dma((2, 3)),

time: 54.8 us -> 54.8 us (level)
  no operation moved by 1% of the time
where the time goes in v5:
time: 54.8 us
  Pallas kernels  53.9 us (98%)
  local copies, waits for them, and re-layouts  0.84 us (2%)
    pallas_call x1, Pallas kernels, local(): pl.pallas_call(functools.partial(kernel, nx, nz, ny), out_shape=pltpu.VME...  53.9 us

profile of v5, /device:TPU:1, one launch (start us, length us, event | category | flops | bytes accessed | tf_op | source)
XLA Modules:
  0.0 54.8 jit_solution(9262261484799527834)
XLA Ops:
  0.0 53.9 %ssd_layer.1 = bf16[128,2560]{1,0:T(8,128)(2,1)S(1)} custom-call(bf16[512,1280]{1,0:T(8,128)(2,1)} %x_hbm.1, bf16[512,1280]{1,0:T(8,128)(2,1)} %g_hbm.1, bf16[512,128]{1,0:T(8,128)(2,1)} %b_hbm.1, bf16[512,128]{1,0:T(8,128)(2,1)} %c_hbm.1, f32[20,512]{1,0:T(8,128)} %st_hbm.1, f32[1,20]{1,0:T(1,128)} %bitcast.4, f32[1,20]{1,0:T(1,128)} %bitcast.5, ...), custom_call_target="tpu_custom_call" | custom-call | tf_op jit(solution)/shard_map/ssd_layer/pallas_call | solution.py:720
  53.9 0.8 %copy.13 = bf16[128,2560]{1,0:T(8,128)(2,1)} copy(bf16[128,2560]{1,0:T(8,128)(2,1)S(1)} %ssd_layer.1) | data formatting | bytes 1310720

commit v6 on v5

--- a/solution.py
+++ b/solution.py
@@ -471,7 +471,6 @@
             else:
                 brecv[z, :, cols] = value
 
-    other_lanes = pl.ds(pl.multiple_of(others, LANE), side_width)
     final_copies = []
     for g, cols in enumerate(groups):
         own_lanes = pl.ds(pl.multiple_of(mine + cols.start, LANE), cols.stop - cols.start)
@@ -551,15 +550,19 @@
     squares = jnp.zeros((part, 1), F32)
     for cut in cuts:
         squares = squares + hidden_columns(far, lanes(mine, cut))
-    for copy in final_copies:
-        copy.wait_recv()
-    for j in range(nz):
-        rows = slice(j * sr, (j + 1) * sr)
-        sp_ref[rows, other_lanes] = (row_ref[8:9, other_lanes] * frecv[j].astype(F32)).astype(
-            BF16
-        )
-    for cut in cuts:
-        squares = squares + hidden_columns(far, lanes(others, cut))
+    for g, cols in enumerate(groups):
+        size = cols.stop - cols.start
+        for copy in final_copies[g * nz : (g + 1) * nz]:
+            copy.wait_recv()
+        other_lanes = pl.ds(pl.multiple_of(others + cols.start, LANE), size)
+        for j in range(nz):
+            rows = slice(j * sr, (j + 1) * sr)
+            sp_ref[rows, other_lanes] = (
+                row_ref[8:9, other_lanes] * frecv[j, :, cols].astype(F32)
+            ).astype(BF16)
+        for c in range(0, size, 256):
+            cut = (cols.start + c, min(256, size - c))
+            squares = squares + hidden_columns(far, lanes(others, cut))
     loads[5].wait()
     up, down = in_y[1], in_y[ny - 1]
     spans = ((0, 256), (256, half))

time: 54.8 us -> 54.9 us (level)
  no operation moved by 1% of the time
where the time goes in v6:
time: 54.9 us; the launch traced here: 54.8 us
  Pallas kernels  54 us (98%)
  local copies, waits for them, and re-layouts  0.84 us (2%)
    pallas_call x1, Pallas kernels, local(): pl.pallas_call(functools.partial(kernel, nx, nz, ny), out_shape=pltpu.VME...  54 us

profile of v6, /device:TPU:1, one launch (start us, length us, event | category | flops | bytes accessed | tf_op | source)
XLA Modules:
  0.0 54.8 jit_solution(9558990212909985094)
XLA Ops:
  0.0 54.0 %ssd_layer.1 = bf16[128,2560]{1,0:T(8,128)(2,1)S(1)} custom-call(bf16[512,1280]{1,0:T(8,128)(2,1)} %x_hbm.1, bf16[512,1280]{1,0:T(8,128)(2,1)} %g_hbm.1, bf16[512,128]{1,0:T(8,128)(2,1)} %b_hbm.1, bf16[512,128]{1,0:T(8,128)(2,1)} %c_hbm.1, f32[20,512]{1,0:T(8,128)} %st_hbm.1, f32[1,20]{1,0:T(1,128)} %bitcast.4, f32[1,20]{1,0:T(1,128)} %bitcast.5, ...), custom_call_target="tpu_custom_call" | custom-call | tf_op jit(solution)/shard_map/ssd_layer/pallas_call | solution.py:723
  54.0 0.8 %copy.13 = bf16[128,2560]{1,0:T(8,128)(2,1)} copy(bf16[128,2560]{1,0:T(8,128)(2,1)S(1)} %ssd_layer.1) | data formatting | bytes 1310720
